TPU v7x, 128 devices: a whole 4x4x4 slice. The times are simulated.
128 devices in a mesh: sys: 8 (over x, core), slab: 16 (over z, y).
Axes of the slice: x: 4, y: 4, z: 4, core: 2. Of those that a mesh axis runs over, the one named last changes fastest.
Arguments:
- right_side: float32 [256, 1024, 128], P('slab', 'sys'), parts along dimension 1, may hold values from -8 to 8
- diagonal: float32 [256, 1024, 128], P('slab', 'sys'), parts along dimension 1, may hold values from 0.25 to 2
Outputs:
- solution_field: float32 [256, 1024, 128], P('slab', 'sys'), parts along dimension 1
- residual: float32 [256, 1024, 128], P('slab', 'sys'), parts along dimension 1
There are 8 independent parts, one for each index of `sys`. A program takes and returns all parts, laid end to end along the dimension named above; each array names one. Nothing has to cross between parts.
All inputs are finite; a program needn't handle non-finite values.
Results may differ from a plain program's by a relative error of at most 0.0003.
Values sent between devices are 32-bit elements; how exact they have to be, the bound alone decides.
A program may use at most 64 MiB of HBM per device.

v0:
```python
import jax
import jax.numpy as jnp
from jax import lax
from jax.sharding import PartitionSpec as P

ITERS = 10


def with_halo(cells, sides, width):
    for axis, dim in sides:
        count = lax.axis_size(axis)
        ends = count - 1
        head = lax.slice_in_dim(cells, 0, width, axis=dim)
        tail = lax.slice_in_dim(cells, cells.shape[dim] - width, cells.shape[dim], axis=dim)
        cells = jnp.concatenate(
            [
                lax.ppermute(tail, axis, [(i, (i + 1) % count) for i in range(ends)]),
                cells,
                lax.ppermute(head, axis, [((i + 1) % count, i) for i in range(ends)]),
            ],
            axis=dim,
        )
    return cells


def copy_for_each(shard, axis):
    copies = jnp.broadcast_to(shard, (lax.axis_size(axis), *shard.shape))
    return lax.all_to_all(copies, axis, split_axis=0, concat_axis=0, tiled=True)


def of_everyone(shard, axis):
    return copy_for_each(shard, axis).sum(axis=0)


def together(arrays, axis):
    line, at, outs = (jnp.concatenate([a.reshape(-1) for a in arrays]), 0, [])
    running = of_everyone(line, axis)
    for a in arrays:
        outs.append(running[at : at + a.size].reshape(a.shape))
        at += a.size
    return tuple(outs)


def operate(values, diagonal):
    padded = with_halo(values, (("slab", 0),), 1)
    beside = padded[2:] + padded[:-2]
    beside = beside + jnp.pad(values[:, 1:], ((0, 0), (0, 1), (0, 0)))
    beside = beside + jnp.pad(values[:, :-1], ((0, 0), (1, 0), (0, 0)))
    beside = beside + jnp.pad(values[:, :, 1:], ((0, 0), (0, 0), (0, 1)))
    beside = beside + jnp.pad(values[:, :, :-1], ((0, 0), (0, 0), (1, 0)))
    return (6.0 + diagonal) * values - beside


def paired_sums(residual, applied):
    return together((jnp.sum(residual * residual), jnp.sum(applied * residual)), "slab")


def local(right_side, diagonal):
    solution_field = jnp.zeros_like(right_side)
    residual = right_side
    applied = operate(residual, diagonal)
    direction = jnp.zeros_like(right_side)
    along = jnp.zeros_like(right_side)
    further_dir = jnp.zeros_like(right_side)
    norm_old = jnp.float32(1.0)
    step_old = jnp.float32(1.0)
    for iteration in range(ITERS):
        norm_now, product = paired_sums(residual, applied)
        if iteration + 1 < ITERS:
            further = operate(applied, diagonal)
        if iteration == 0:
            scaling = jnp.float32(0.0)
            step_size = norm_now / product
        else:
            scaling = norm_now / norm_old
            step_size = norm_now / (product - scaling * norm_now / step_old)
        direction = residual + scaling * direction
        along = applied + scaling * along
        solution_field = solution_field + step_size * direction
        residual = residual - step_size * along
        if iteration + 1 < ITERS:
            further_dir = further + scaling * further_dir
            applied = applied - step_size * further_dir
        norm_old = norm_now
        step_old = step_size
    return (solution_field, residual)


def solution(mesh):
    placed = (P("slab", "sys", None), P("slab", "sys", None))
    return jax.shard_map(
        local,
        mesh=mesh,
        in_specs=placed,
        out_specs=(P("slab", "sys", None), P("slab", "sys", None)),
        check_vma=False,
    )
```

profile of v0, /device:TPU:0, one launch (start us, length us, event | category | flops | bytes accessed | tf_op | source)
XLA Modules:
  0.0 321.2 jit_solution(2154432051947620180)
XLA Ops:
  2.8 4.7 %collective-permute-start.1 = (f32[1,128,128]{2,1,0:T(8,128)S(1)}, f32[1,128,128]{2,1,0:T(8,128)S(1)}, u32[]{:S(2)}, u32[]{:S(2)}) collective-permute-start(f32[1,128,128]{2,1,0:T(8,128)S(1)} %get-tuple-element.107), channel_id=1, source_target_pairs={{0,1},{1,2},{2,3},{3,4},{4,5},{5,6},{6,7},{7,8},{8,9},{9,10},{10,1... | collective-permute-start | bytes 196616 | tf_op jit(solution)/shard_map/ppermute | solution.py:17
  17.1 9.9 %all-to-all-start = ((f32[16,1,2]{2,1,0:T(1,128)}), f32[16,1,2]{2,1,0:T(1,128)S(1)}, u32[]{:S(2)}, u32[]{:S(2)}) async-start(f32[16,1,2]{2,1,0:T(1,128)} %broadcast_in_dim.30), calls=%async_computation | async-start | bytes 16384 | tf_op jit(solution)/shard_map/all_to_all | solution.py:28
  28.4 4.5 %collective-permute-start.3 = (f32[1,128,128]{2,1,0:T(8,128)S(1)}, f32[1,128,128]{2,1,0:T(8,128)S(1)}, u32[]{:S(2)}, u32[]{:S(2)}) collective-permute-start(f32[1,128,128]{2,1,0:T(8,128)S(1)} %get-tuple-element.101), channel_id=1, source_target_pairs={{0,1},{1,2},{2,3},{3,4},{4,5},{5,6},{6,7},{7,8},{8,9},{9,10},{10,1... | collective-permute-start | bytes 196616 | tf_op jit(solution)/shard_map/ppermute | solution.py:17
  36.8 5.2 %multiply_reduce_fusion.17 = (f32[]{:T(128)}, f32[]{:T(128)}, f32[16,128,128]{2,1,0:T(8,128)S(1)}, f32[16,128,128]{2,1,0:T(8,128)}, f32[16,128,128]{2,1,0:T(8,128)}) fusion(f32[16,128,128]{2,1,0:T(8,128)S(1)} %get-tuple-element.51, f32[]{:T(128)S(6)} %div.84, f32[16,128,127]{2,1,0:T(8,128)} %get-tuple-element.105, f32[16,128,127]{2,1,0:T(8,128)} %get-tuple-element.104, ...), kind=kLoop, calls=%fused_computation.133 | loop fusion | flops 4718590 | bytes 10584076 | tf_op jit(solution)/shard_map/reduce_sum | solution.py:55
  47.1 7.9 %all-to-all-start.1 = ((f32[16,1,2]{2,1,0:T(1,128)}), f32[16,1,2]{2,1,0:T(1,128)S(1)}, u32[]{:S(2)}, u32[]{:S(2)}) async-start(f32[16,1,2]{2,1,0:T(1,128)} %broadcast_in_dim.31), calls=%async_computation.1 | async-start | bytes 16384 | tf_op jit(solution)/shard_map/all_to_all | solution.py:28
  67.4 5.7 %multiply_reduce_fusion.15 = (f32[]{:T(128)}, f32[]{:T(128)}, f32[16,128,128]{2,1,0:T(8,128)S(1)}, f32[16,128,128]{2,1,0:T(8,128)}, f32[16,128,128]{2,1,0:T(8,128)}) fusion(f32[16,128,128]{2,1,0:T(8,128)S(1)} %get-tuple-element.48, f32[]{:T(128)S(6)} %div.87, f32[16,128,128]{2,1,0:T(8,128)} %get-tuple-element.49, f32[]{:T(128)S(6)} %div.85, ...), kind=kLoop, calls=%fused_computation.128 | loop fusion | flops 5767166 | bytes 12681232 | tf_op jit(solution)/shard_map/reduce_sum | solution.py:55
  78.3 7.5 %all-to-all-start.2 = ((f32[16,1,2]{2,1,0:T(1,128)}), f32[16,1,2]{2,1,0:T(1,128)S(1)}, u32[]{:S(2)}, u32[]{:S(2)}) async-start(f32[16,1,2]{2,1,0:T(1,128)} %broadcast_in_dim.32), calls=%async_computation.2 | async-start | bytes 16384 | tf_op jit(solution)/shard_map/all_to_all | solution.py:28
  87.1 4.5 %collective-permute-start.7 = (f32[1,128,128]{2,1,0:T(8,128)S(1)}, f32[1,128,128]{2,1,0:T(8,128)S(1)}, u32[]{:S(2)}, u32[]{:S(2)}) collective-permute-start(f32[1,128,128]{2,1,0:T(8,128)S(1)} %get-tuple-element.89), channel_id=1, source_target_pairs={{0,1},{1,2},{2,3},{3,4},{4,5},{5,6},{6,7},{7,8},{8,9},{9,10},{10,1... | collective-permute-start | bytes 196616 | tf_op jit(solution)/shard_map/ppermute | solution.py:17
  97.7 7.8 %multiply_reduce_fusion.13 = (f32[]{:T(128)}, f32[]{:T(128)}, f32[16,128,128]{2,1,0:T(8,128)S(1)}, f32[16,128,128]{2,1,0:T(8,128)}, f32[16,128,128]{2,1,0:T(8,128)}, /*index=5*/f32[16,128,128]{2,1,0:T(8,128)}) fusion(f32[16,128,128]{2,1,0:T(8,128)} %copy-done.4, f32[]{:T(128)S(6)} %div.90, f32[16,128,128]{2,1,0:T(8,128)} %get-tuple-element.46, f32[]{:T(128)S(6)} %div.88, ...), kind=kLoop, calls=%fused_computation.123 | loop fusion | flops 6291454 | bytes 14778388 | tf_op jit(solution)/shard_map/reduce_sum | solution.py:55
  110.6 7.3 %all-to-all-start.3 = ((f32[16,1,2]{2,1,0:T(1,128)}), f32[16,1,2]{2,1,0:T(1,128)S(1)}, u32[]{:S(2)}, u32[]{:S(2)}) async-start(f32[16,1,2]{2,1,0:T(1,128)} %broadcast_in_dim.33), calls=%async_computation.3 | async-start | bytes 16384 | tf_op jit(solution)/shard_map/all_to_all | solution.py:28
  130.0 5.8 %multiply_reduce_fusion.11 = (f32[]{:T(128)}, f32[]{:T(128)}, f32[16,128,128]{2,1,0:T(8,128)S(1)}, f32[16,128,128]{2,1,0:T(8,128)}, f32[16,128,128]{2,1,0:T(8,128)}) fusion(f32[16,128,128]{2,1,0:T(8,128)S(1)} %get-tuple-element.41, f32[]{:T(128)S(6)} %div.93, f32[16,128,128]{2,1,0:T(8,128)} %get-tuple-element.42, f32[]{:T(128)S(6)} %div.91, ...), kind=kLoop, calls=%fused_computation.118 | loop fusion | flops 5767166 | bytes 12681232 | tf_op jit(solution)/shard_map/reduce_sum | solution.py:55
  140.8 7.3 %all-to-all-start.4 = ((f32[16,1,2]{2,1,0:T(1,128)}), f32[16,1,2]{2,1,0:T(1,128)S(1)}, u32[]{:S(2)}, u32[]{:S(2)}) async-start(f32[16,1,2]{2,1,0:T(1,128)} %broadcast_in_dim.34), calls=%async_computation.4 | async-start | bytes 16384 | tf_op jit(solution)/shard_map/all_to_all | solution.py:28
  149.5 4.7 %collective-permute-start.11 = (f32[1,128,128]{2,1,0:T(8,128)S(1)}, f32[1,128,128]{2,1,0:T(8,128)S(1)}, u32[]{:S(2)}, u32[]{:S(2)}) collective-permute-start(f32[1,128,128]{2,1,0:T(8,128)S(1)} %get-tuple-element.77), channel_id=1, source_target_pairs={{0,1},{1,2},{2,3},{3,4},{4,5},{5,6},{6,7},{7,8},{8,9},{9,10},{10,1... | collective-permute-start | bytes 196616 | tf_op jit(solution)/shard_map/ppermute | solution.py:17
  160.2 7.7 %multiply_reduce_fusion.9 = (f32[]{:T(128)}, f32[]{:T(128)}, f32[16,128,128]{2,1,0:T(8,128)S(1)}, f32[16,128,128]{2,1,0:T(8,128)}, f32[16,128,128]{2,1,0:T(8,128)}, /*index=5*/f32[16,128,128]{2,1,0:T(8,128)}) fusion(f32[16,128,128]{2,1,0:T(8,128)} %copy-done.5, f32[]{:T(128)S(6)} %div.96, f32[16,128,128]{2,1,0:T(8,128)} %get-tuple-element.39, f32[]{:T(128)S(6)} %div.94, ...), kind=kLoop, calls=%fused_computation.113 | loop fusion | flops 6291454 | bytes 14778388 | tf_op jit(solution)/shard_map/reduce_sum | solution.py:55
  173.1 7.6 %all-to-all-start.5 = ((f32[16,1,2]{2,1,0:T(1,128)}), f32[16,1,2]{2,1,0:T(1,128)S(1)}, u32[]{:S(2)}, u32[]{:S(2)}) async-start(f32[16,1,2]{2,1,0:T(1,128)} %broadcast_in_dim.35), calls=%async_computation.5 | async-start | bytes 16384 | tf_op jit(solution)/shard_map/all_to_all | solution.py:28
  192.8 5.8 %multiply_reduce_fusion.7 = (f32[]{:T(128)}, f32[]{:T(128)}, f32[16,128,128]{2,1,0:T(8,128)S(1)}, f32[16,128,128]{2,1,0:T(8,128)}, f32[16,128,128]{2,1,0:T(8,128)}) fusion(f32[16,128,128]{2,1,0:T(8,128)S(1)} %get-tuple-element.34, f32[]{:T(128)S(6)} %div.99, f32[16,128,128]{2,1,0:T(8,128)} %get-tuple-element.35, f32[]{:T(128)S(6)} %div.97, ...), kind=kLoop, calls=%fused_computation.108 | loop fusion | flops 5767166 | bytes 12681232 | tf_op jit(solution)/shard_map/reduce_sum | solution.py:55
  203.9 7.3 %all-to-all-start.6 = ((f32[16,1,2]{2,1,0:T(1,128)}), f32[16,1,2]{2,1,0:T(1,128)S(1)}, u32[]{:S(2)}, u32[]{:S(2)}) async-start(f32[16,1,2]{2,1,0:T(1,128)} %broadcast_in_dim.36), calls=%async_computation.6 | async-start | bytes 16384 | tf_op jit(solution)/shard_map/all_to_all | solution.py:28
  223.4 8.1 %multiply_reduce_fusion.5 = (f32[]{:T(128)}, f32[]{:T(128)}, f32[16,128,128]{2,1,0:T(8,128)S(1)}, f32[16,128,128]{2,1,0:T(8,128)}, f32[16,128,128]{2,1,0:T(8,128)}, /*index=5*/f32[16,128,128]{2,1,0:T(8,128)}) fusion(f32[16,128,128]{2,1,0:T(8,128)} %copy-done.6, f32[]{:T(128)S(6)} %div.102, f32[16,128,128]{2,1,0:T(8,128)} %get-tuple-element.32, ...), kind=kLoop, calls=%fused_computation.103 | loop fusion | flops 6291454 | bytes 14778388 | tf_op jit(solution)/shard_map/reduce_sum | solution.py:55
  236.7 7.5 %all-to-all-start.7 = ((f32[16,1,2]{2,1,0:T(1,128)}), f32[16,1,2]{2,1,0:T(1,128)S(1)}, u32[]{:S(2)}, u32[]{:S(2)}) async-start(f32[16,1,2]{2,1,0:T(1,128)} %broadcast_in_dim.37), calls=%async_computation.7 | async-start | bytes 16384 | tf_op jit(solution)/shard_map/all_to_all | solution.py:28
  256.1 5.6 %multiply_reduce_fusion.3 = (f32[]{:T(128)}, f32[]{:T(128)}, f32[16,128,128]{2,1,0:T(8,128)S(1)}, f32[16,128,128]{2,1,0:T(8,128)}, f32[16,128,128]{2,1,0:T(8,128)}) fusion(f32[16,128,128]{2,1,0:T(8,128)S(1)} %get-tuple-element.27, f32[]{:T(128)S(6)} %div.105, f32[16,128,128]{2,1,0:T(8,128)} %get-tuple-element.28, f32[]{:T(128)S(6)} %div.103, ...), kind=kLoop, calls=%fused_computation.98 | loop fusion | flops 5767166 | bytes 12681232 | tf_op jit(solution)/shard_map/reduce_sum | solution.py:55
  266.8 7.5 %all-to-all-start.8 = ((f32[16,1,2]{2,1,0:T(1,128)}), f32[16,1,2]{2,1,0:T(1,128)S(1)}, u32[]{:S(2)}, u32[]{:S(2)}) async-start(f32[16,1,2]{2,1,0:T(1,128)} %broadcast_in_dim.38), calls=%async_computation.8 | async-start | bytes 16384 | tf_op jit(solution)/shard_map/all_to_all | solution.py:28
  286.0 7.3 %multiply_reduce_fusion.1 = (f32[]{:T(128)}, f32[]{:T(128)}, f32[16,128,128]{2,1,0:T(8,128)}, f32[16,128,128]{2,1,0:T(8,128)}) fusion(f32[16,128,128]{2,1,0:T(8,128)} %get-tuple-element.26, f32[]{:T(128)S(6)} %div.108, f32[16,128,128]{2,1,0:T(8,128)} %copy-done.7, f32[16,128,128]{2,1,0:T(8,128)} %get-tuple-element.25, f32[]{:T(128)S(6)} %div.106, ...), kind=kLoop, calls=%fused_computation.93 | loop fusion | flops 6291454 | bytes 12681236 | tf_op jit(solution)/shard_map/reduce_sum | solution.py:55
  294.6 14.7 %all_to_all.60 = f32[16,1,2]{2,1,0:T(1,128)S(1)} all-to-all(f32[16,1,2]{2,1,0:T(1,128)S(1)} %broadcast_in_dim.39), channel_id=1, replica_groups=mesh['sys'=8,'slab'=16] {'slab'}, dimensions={0} | all-to-all | bytes 256 | tf_op jit(solution)/shard_map/all_to_all | solution.py:28
  313.7 6.2 %multiply_add_fusion = f32[16,128,128]{2,1,0:T(8,128)} fusion(f32[16,128,128]{2,1,0:T(8,128)} %get-tuple-element.26, f32[16,128,128]{2,1,0:T(8,128)} %get-tuple-element.29, f32[16,128,128]{2,1,0:T(8,128)} %get-tuple-element.33, f32[16,128,128]{2,1,0:T(8,128)} %get-tuple-element.36, f32[16,128,128]{2,1,0:T(8,128)} %get-tuple-element.40, ...), kind=kLoop, calls=%fused_computation.91 | loop fusion | flops 10223616 | bytes 11534412 | tf_op jit(solution)/shard_map/add | solution.py:79
  (145 shorter events, 115.7 us)
Async XLA Ops:
  17.1 17.5 %all-to-all-start = ((f32[16,1,2]{2,1,0:T(1,128)}), f32[16,1,2]{2,1,0:T(1,128)S(1)}, u32[]{:S(2)}, u32[]{:S(2)}) async-start(f32[16,1,2]{2,1,0:T(1,128)} %broadcast_in_dim.30), calls=%async_computation | async-start | bytes 16384 | tf_op jit(solution)/shard_map/all_to_all | solution.py:28
  47.1 15.4 %all-to-all-start.1 = ((f32[16,1,2]{2,1,0:T(1,128)}), f32[16,1,2]{2,1,0:T(1,128)S(1)}, u32[]{:S(2)}, u32[]{:S(2)}) async-start(f32[16,1,2]{2,1,0:T(1,128)} %broadcast_in_dim.31), calls=%async_computation.1 | async-start | bytes 16384 | tf_op jit(solution)/shard_map/all_to_all | solution.py:28
  55.0 12.4 %collective-permute-start.4 = (f32[1,128,128]{2,1,0:T(8,128)S(1)}, f32[1,128,128]{2,1,0:T(8,128)S(1)}, u32[]{:S(2)}, u32[]{:S(2)}) collective-permute-start(f32[1,128,128]{2,1,0:T(8,128)S(1)} %get-tuple-element.94), channel_id=1, source_target_pairs={{1,0},{2,1},{3,2},{4,3},{5,4},{6,5},{7,6},{8,7},{9,8},{10,9},{11,1... | collective-permute-start | bytes 196616 | tf_op jit(solution)/shard_map/ppermute | solution.py:19
  56.3 11.1 %collective-permute-start.5 = (f32[1,128,128]{2,1,0:T(8,128)S(1)}, f32[1,128,128]{2,1,0:T(8,128)S(1)}, u32[]{:S(2)}, u32[]{:S(2)}) collective-permute-start(f32[1,128,128]{2,1,0:T(8,128)S(1)} %get-tuple-element.95), channel_id=1, source_target_pairs={{0,1},{1,2},{2,3},{3,4},{4,5},{5,6},{6,7},{7,8},{8,9},{9,10},{10,1... | collective-permute-start | bytes 196616 | tf_op jit(solution)/shard_map/ppermute | solution.py:17
  78.3 15.1 %all-to-all-start.2 = ((f32[16,1,2]{2,1,0:T(1,128)}), f32[16,1,2]{2,1,0:T(1,128)S(1)}, u32[]{:S(2)}, u32[]{:S(2)}) async-start(f32[16,1,2]{2,1,0:T(1,128)} %broadcast_in_dim.32), calls=%async_computation.2 | async-start | bytes 16384 | tf_op jit(solution)/shard_map/all_to_all | solution.py:28
  85.8 11.8 %collective-permute-start.6 = (f32[1,128,128]{2,1,0:T(8,128)S(1)}, f32[1,128,128]{2,1,0:T(8,128)S(1)}, u32[]{:S(2)}, u32[]{:S(2)}) collective-permute-start(f32[1,128,128]{2,1,0:T(8,128)S(1)} %get-tuple-element.88), channel_id=1, source_target_pairs={{1,0},{2,1},{3,2},{4,3},{5,4},{6,5},{7,6},{8,7},{9,8},{10,9},{11,1... | collective-permute-start | bytes 196616 | tf_op jit(solution)/shard_map/ppermute | solution.py:19
  87.1 10.6 %collective-permute-start.7 = (f32[1,128,128]{2,1,0:T(8,128)S(1)}, f32[1,128,128]{2,1,0:T(8,128)S(1)}, u32[]{:S(2)}, u32[]{:S(2)}) collective-permute-start(f32[1,128,128]{2,1,0:T(8,128)S(1)} %get-tuple-element.89), channel_id=1, source_target_pairs={{0,1},{1,2},{2,3},{3,4},{4,5},{5,6},{6,7},{7,8},{8,9},{9,10},{10,1... | collective-permute-start | bytes 196616 | tf_op jit(solution)/shard_map/ppermute | solution.py:17
  110.6 14.9 %all-to-all-start.3 = ((f32[16,1,2]{2,1,0:T(1,128)}), f32[16,1,2]{2,1,0:T(1,128)S(1)}, u32[]{:S(2)}, u32[]{:S(2)}) async-start(f32[16,1,2]{2,1,0:T(1,128)} %broadcast_in_dim.33), calls=%async_computation.3 | async-start | bytes 16384 | tf_op jit(solution)/shard_map/all_to_all | solution.py:28
  117.9 12.1 %collective-permute-start.8 = (f32[1,128,128]{2,1,0:T(8,128)S(1)}, f32[1,128,128]{2,1,0:T(8,128)S(1)}, u32[]{:S(2)}, u32[]{:S(2)}) collective-permute-start(f32[1,128,128]{2,1,0:T(8,128)S(1)} %get-tuple-element.82), channel_id=1, source_target_pairs={{1,0},{2,1},{3,2},{4,3},{5,4},{6,5},{7,6},{8,7},{9,8},{10,9},{11,1... | collective-permute-start | bytes 196616 | tf_op jit(solution)/shard_map/ppermute | solution.py:19
  119.2 10.8 %collective-permute-start.9 = (f32[1,128,128]{2,1,0:T(8,128)S(1)}, f32[1,128,128]{2,1,0:T(8,128)S(1)}, u32[]{:S(2)}, u32[]{:S(2)}) collective-permute-start(f32[1,128,128]{2,1,0:T(8,128)S(1)} %get-tuple-element.83), channel_id=1, source_target_pairs={{0,1},{1,2},{2,3},{3,4},{4,5},{5,6},{6,7},{7,8},{8,9},{9,10},{10,1... | collective-permute-start | bytes 196616 | tf_op jit(solution)/shard_map/ppermute | solution.py:17
  140.8 14.8 %all-to-all-start.4 = ((f32[16,1,2]{2,1,0:T(1,128)}), f32[16,1,2]{2,1,0:T(1,128)S(1)}, u32[]{:S(2)}, u32[]{:S(2)}) async-start(f32[16,1,2]{2,1,0:T(1,128)} %broadcast_in_dim.34), calls=%async_computation.4 | async-start | bytes 16384 | tf_op jit(solution)/shard_map/all_to_all | solution.py:28
  148.2 12.1 %collective-permute-start.10 = (f32[1,128,128]{2,1,0:T(8,128)S(1)}, f32[1,128,128]{2,1,0:T(8,128)S(1)}, u32[]{:S(2)}, u32[]{:S(2)}) collective-permute-start(f32[1,128,128]{2,1,0:T(8,128)S(1)} %get-tuple-element.76), channel_id=1, source_target_pairs={{1,0},{2,1},{3,2},{4,3},{5,4},{6,5},{7,6},{8,7},{9,8},{10,9},{11,1... | collective-permute-start | bytes 196616 | tf_op jit(solution)/shard_map/ppermute | solution.py:19
  149.5 10.8 %collective-permute-start.11 = (f32[1,128,128]{2,1,0:T(8,128)S(1)}, f32[1,128,128]{2,1,0:T(8,128)S(1)}, u32[]{:S(2)}, u32[]{:S(2)}) collective-permute-start(f32[1,128,128]{2,1,0:T(8,128)S(1)} %get-tuple-element.77), channel_id=1, source_target_pairs={{0,1},{1,2},{2,3},{3,4},{4,5},{5,6},{6,7},{7,8},{8,9},{9,10},{10,1... | collective-permute-start | bytes 196616 | tf_op jit(solution)/shard_map/ppermute | solution.py:17
  173.1 15.2 %all-to-all-start.5 = ((f32[16,1,2]{2,1,0:T(1,128)}), f32[16,1,2]{2,1,0:T(1,128)S(1)}, u32[]{:S(2)}, u32[]{:S(2)}) async-start(f32[16,1,2]{2,1,0:T(1,128)} %broadcast_in_dim.35), calls=%async_computation.5 | async-start | bytes 16384 | tf_op jit(solution)/shard_map/all_to_all | solution.py:28
  180.7 12.1 %collective-permute-start.12 = (f32[1,128,128]{2,1,0:T(8,128)S(1)}, f32[1,128,128]{2,1,0:T(8,128)S(1)}, u32[]{:S(2)}, u32[]{:S(2)}) collective-permute-start(f32[1,128,128]{2,1,0:T(8,128)S(1)} %get-tuple-element.70), channel_id=1, source_target_pairs={{1,0},{2,1},{3,2},{4,3},{5,4},{6,5},{7,6},{8,7},{9,8},{10,9},{11,1... | collective-permute-start | bytes 196616 | tf_op jit(solution)/shard_map/ppermute | solution.py:19
  182.0 10.8 %collective-permute-start.13 = (f32[1,128,128]{2,1,0:T(8,128)S(1)}, f32[1,128,128]{2,1,0:T(8,128)S(1)}, u32[]{:S(2)}, u32[]{:S(2)}) collective-permute-start(f32[1,128,128]{2,1,0:T(8,128)S(1)} %get-tuple-element.71), channel_id=1, source_target_pairs={{0,1},{1,2},{2,3},{3,4},{4,5},{5,6},{6,7},{7,8},{8,9},{9,10},{10,1... | collective-permute-start | bytes 196616 | tf_op jit(solution)/shard_map/ppermute | solution.py:17
  203.9 14.7 %all-to-all-start.6 = ((f32[16,1,2]{2,1,0:T(1,128)}), f32[16,1,2]{2,1,0:T(1,128)S(1)}, u32[]{:S(2)}, u32[]{:S(2)}) async-start(f32[16,1,2]{2,1,0:T(1,128)} %broadcast_in_dim.36), calls=%async_computation.6 | async-start | bytes 16384 | tf_op jit(solution)/shard_map/all_to_all | solution.py:28
  211.2 12.2 %collective-permute-start.14 = (f32[1,128,128]{2,1,0:T(8,128)S(1)}, f32[1,128,128]{2,1,0:T(8,128)S(1)}, u32[]{:S(2)}, u32[]{:S(2)}) collective-permute-start(f32[1,128,128]{2,1,0:T(8,128)S(1)} %get-tuple-element.64), channel_id=1, source_target_pairs={{1,0},{2,1},{3,2},{4,3},{5,4},{6,5},{7,6},{8,7},{9,8},{10,9},{11,1... | collective-permute-start | bytes 196616 | tf_op jit(solution)/shard_map/ppermute | solution.py:19
  212.5 10.9 %collective-permute-start.15 = (f32[1,128,128]{2,1,0:T(8,128)S(1)}, f32[1,128,128]{2,1,0:T(8,128)S(1)}, u32[]{:S(2)}, u32[]{:S(2)}) collective-permute-start(f32[1,128,128]{2,1,0:T(8,128)S(1)} %get-tuple-element.65), channel_id=1, source_target_pairs={{0,1},{1,2},{2,3},{3,4},{4,5},{5,6},{6,7},{7,8},{8,9},{9,10},{10,1... | collective-permute-start | bytes 196616 | tf_op jit(solution)/shard_map/ppermute | solution.py:17
  236.7 14.9 %all-to-all-start.7 = ((f32[16,1,2]{2,1,0:T(1,128)}), f32[16,1,2]{2,1,0:T(1,128)S(1)}, u32[]{:S(2)}, u32[]{:S(2)}) async-start(f32[16,1,2]{2,1,0:T(1,128)} %broadcast_in_dim.37), calls=%async_computation.7 | async-start | bytes 16384 | tf_op jit(solution)/shard_map/all_to_all | solution.py:28
  244.2 11.9 %collective-permute-start.16 = (f32[1,128,128]{2,1,0:T(8,128)S(1)}, f32[1,128,128]{2,1,0:T(8,128)S(1)}, u32[]{:S(2)}, u32[]{:S(2)}) collective-permute-start(f32[1,128,128]{2,1,0:T(8,128)S(1)} %get-tuple-element.58), channel_id=1, source_target_pairs={{1,0},{2,1},{3,2},{4,3},{5,4},{6,5},{7,6},{8,7},{9,8},{10,9},{11,1... | collective-permute-start | bytes 196616 | tf_op jit(solution)/shard_map/ppermute | solution.py:19
  245.5 10.6 %collective-permute-start.17 = (f32[1,128,128]{2,1,0:T(8,128)S(1)}, f32[1,128,128]{2,1,0:T(8,128)S(1)}, u32[]{:S(2)}, u32[]{:S(2)}) collective-permute-start(f32[1,128,128]{2,1,0:T(8,128)S(1)} %get-tuple-element.59), channel_id=1, source_target_pairs={{0,1},{1,2},{2,3},{3,4},{4,5},{5,6},{6,7},{7,8},{8,9},{9,10},{10,1... | collective-permute-start | bytes 196616 | tf_op jit(solution)/shard_map/ppermute | solution.py:17
  266.8 15.1 %all-to-all-start.8 = ((f32[16,1,2]{2,1,0:T(1,128)}), f32[16,1,2]{2,1,0:T(1,128)S(1)}, u32[]{:S(2)}, u32[]{:S(2)}) async-start(f32[16,1,2]{2,1,0:T(1,128)} %broadcast_in_dim.38), calls=%async_computation.8 | async-start | bytes 16384 | tf_op jit(solution)/shard_map/all_to_all | solution.py:28
  274.2 11.8 %collective-permute-start.18 = (f32[1,128,128]{2,1,0:T(8,128)S(1)}, f32[1,128,128]{2,1,0:T(8,128)S(1)}, u32[]{:S(2)}, u32[]{:S(2)}) collective-permute-start(f32[1,128,128]{2,1,0:T(8,128)S(1)} %get-tuple-element.52), channel_id=1, source_target_pairs={{1,0},{2,1},{3,2},{4,3},{5,4},{6,5},{7,6},{8,7},{9,8},{10,9},{11,1... | collective-permute-start | bytes 196616 | tf_op jit(solution)/shard_map/ppermute | solution.py:19
  (19 other events, 199.4 us)
where the time goes:
time: 323 us; the launch traced here: 321 us
  starting transfers between devices  129 us (40%)
  other arithmetic  81 us (25%)
  local copies, waits for them, and re-layouts  44.7 us (14%)
  between operations  37.5 us (12%)
  waiting for transfers between devices  14.8 us (5%)
  blocking collectives  14.7 us (5%)
    all_to_all x9, starting transfers between devices, copy_for_each(): return lax.all_to_all(copies, axis, split_axis=0, concat_axis=0, tiled=True)  69.8 us
    reduce_sum x10, other arithmetic, paired_sums(): jnp.sum(residual * residual)  60.3 us
    ppermute x10, starting transfers between devices, with_halo(): lax.ppermute(tail, axis, [(i, (i + 1) % count) for i in range(ends)])  45.8 us
    slice x10, local copies, waits for them, and re-layouts, operate(): beside = beside + jnp.pad(values[:, :, 1:], ((0, 0), (0, 0), (0, 1)))  16.9 us
    all_to_all x9, waiting for transfers between devices, copy_for_each(): return lax.all_to_all(copies, axis, split_axis=0, concat_axis=0, tiled=True)  14.8 us
    all_to_all x1, blocking collectives, copy_for_each(): return lax.all_to_all(copies, axis, split_axis=0, concat_axis=0, tiled=True)  14.7 us
    slice x10, local copies, waits for them, and re-layouts, operate(): beside = beside + jnp.pad(values[:, 1:], ((0, 0), (0, 1), (0, 0)))  14.1 us
    concatenate x10, other arithmetic, together(): line, at, outs = (jnp.concatenate([a.reshape(-1) for a in arrays]), 0, [])  13 us
  transfers between devices with their start and end apart: 29, of which 9 were waited for; matrix products, arithmetic and copies ran while one was open for 2% of the time, Pallas kernels for 0%

commit v1 on v0

v1 whole, which is shorter than its diff:
```python
import functools

import jax
import jax.numpy as jnp
import numpy as np
from jax import lax
from jax.experimental import pallas as pl
from jax.experimental.pallas import tpu as pltpu
from jax.sharding import PartitionSpec as P

MID = 7.125
HALF = 6.875
BLOCKS = (3, 3, 4)
STEPS = sum(BLOCKS)
BASES = tuple(int(b) for b in np.cumsum((0,) + BLOCKS[:-1]))
GHOST = max(BLOCKS)
PAD = 8
SLOTS = 8
SHIFT = 32
MESH = pl.DeviceIdType.MESH


def tables():
    n = STEPS
    apply = np.zeros((n + 1, n))
    at_zero = np.zeros(n + 1)
    at_zero[0] = 1.0
    for base, steps in zip(BASES, BLOCKS):
        for j in range(steps):
            i = base + j
            apply[i, i] = MID
            if j == 0:
                apply[i + 1, i] = HALF
                at_zero[i + 1] = -MID / HALF * at_zero[i]
            else:
                apply[i + 1, i] = apply[i - 1, i] = HALF / 2
                at_zero[i + 1] = -2 * MID / HALF * at_zero[i] - at_zero[i - 1]
    divide = np.zeros((n, n + 1))
    divide[:, 1:] = -np.linalg.inv(apply[1:])
    maps = np.concatenate([divide, np.eye(n + 1), at_zero[None]]).T
    sides = np.zeros((24, 128))
    sides[:n, SHIFT : SHIFT + maps.shape[1]] = -maps[:n]
    sides[16:, SHIFT : SHIFT + maps.shape[1]] = maps[n]
    high = sides.astype(np.float32)
    return np.stack([high, (sides - high).astype(np.float32)])


def two_sum(a, b):
    s = a + b
    t = s - a
    return s, (a - (s - t)) + (b - t)


def quick(a, b):
    s = a + b
    return s, b - (s - a)


def halves(a):
    c = a * 4097.0
    h = c - (c - a)
    return h, a - h


def add2(a, b):
    s, e = two_sum(a[0], b[0])
    return quick(s, e + (a[1] + b[1]))


def mul2(a, b):
    p = a[0] * b[0]
    ah, al = halves(a[0])
    bh, bl = halves(b[0])
    e = ((ah * bh - p) + (ah * bl + al * bh)) + al * bl
    return quick(p, e + (a[0] * b[1] + a[1] * b[0]))


def neg2(a):
    return (-a[0], -a[1])


def inverse2(a):
    y = 1.0 / a[0]
    zero = jnp.zeros_like(y)
    p, e = mul2(a, (y, zero))
    return quick(y, y * ((1.0 - p) - e))


def tree2(parts):
    while len(parts) > 1:
        parts = [add2(parts[i], parts[i + 1]) for i in range(0, len(parts) - 1, 2)] + (
            [parts[-1]] if len(parts) % 2 else []
        )
    return parts[0]


def sublanes2(a):
    for shift in (4, 2, 1):
        a = add2(a, tuple(pltpu.roll(v, shift, 0) for v in a))
    return a


def kernel(
    devices,
    right_ref,
    diag_ref,
    table_ref,
    x_ref,
    r_ref,
    V,
    D,
    ACC,
    RED,
    PACK,
    SEND,
    GOT,
    TAB,
    load_sem,
    send_sem,
    recv_sem,
    all_send,
    all_recv,
    store_sem,
):
    planes, rows = right_ref.shape[0], right_ref.shape[1]
    chunks = rows // 8
    me = lax.axis_index("slab")
    below = lax.rem(me + devices - 1, devices)
    above = lax.rem(me + 1, devices)
    has_below = me > 0
    has_above = me < devices - 1
    body = pl.ds(PAD, rows)
    deep = GHOST

    def load(ref, at, first, count, sem):
        return pltpu.make_async_copy(
            ref.at[pl.ds(first, count)], at.at[pl.ds(GHOST + first, count), body], load_sem.at[sem]
        )

    loads = []
    for sem, (ref, at) in enumerate(((right_ref, V.at[0]), (diag_ref, D))):
        loads.append(load(ref, at, 0, deep, 3 * sem))
        loads.append(load(ref, at, planes - deep, deep, 3 * sem + 1))
    for sem, (ref, at) in enumerate(((right_ref, V.at[0]), (diag_ref, D))):
        loads.append(load(ref, at, deep, planes - 2 * deep, 3 * sem + 2))
    table_load = pltpu.make_async_copy(table_ref, TAB, load_sem.at[6])
    for copy in loads:
        copy.start()
    table_load.start()

    barrier = pltpu.get_barrier_semaphore()
    for o in range(1, devices):
        pl.semaphore_signal(
            barrier, inc=1, device_id={"slab": lax.rem(me + o, devices)}, device_id_type=MESH
        )

    zero = jnp.zeros((8, 128), jnp.float32)

    def clear(i, _):
        for k in range(STEPS):
            V[k, i, 0:8, :] = zero
            V[k, i, PAD + rows : PAD + rows + 8, :] = zero
        return 0

    lax.fori_loop(0, planes + 2 * GHOST, clear, 0)

    def clear_ghost(first):
        for base in BASES:
            for i in range(GHOST):
                for c in range(chunks):
                    V[base, first + i, PAD + 8 * c : PAD + 8 * c + 8, :] = zero

    @pl.when(jnp.logical_not(has_below))
    def _():
        clear_ghost(0)

    @pl.when(jnp.logical_not(has_above))
    def _():
        clear_ghost(GHOST + planes)

    def message(array, plane, up, t):
        if up:
            source, target = GHOST + planes - 1 - plane, GHOST - 1 - plane
        else:
            source, target = GHOST + plane, GHOST + planes + plane
        return pltpu.make_async_remote_copy(
            src_ref=array.at[source, body],
            dst_ref=array.at[target, body],
            send_sem=send_sem.at[int(up), t],
            recv_sem=recv_sem.at[int(up), t],
            device_id={"slab": above if up else below},
            device_id_type=MESH,
        )

    numbers = {}
    order = []
    diag_sent = 0
    for index, (base, steps) in enumerate(zip(BASES, BLOCKS)):
        for plane in range(steps):
            order.append((index, "v", plane))
            if index == 0 and plane < steps - 1:
                order.append((index, "d", plane))
        upto = steps - 1 if index + 1 == len(BLOCKS) else max(BLOCKS[: index + 2]) - 1
        for plane in range(max(diag_sent, BLOCKS[0] - 1), upto):
            order.append((index, "d", plane))
        diag_sent = max(upto, diag_sent, BLOCKS[0] - 1)
    for t, (index, kind, plane) in enumerate(order):
        numbers[(kind, plane) if kind == "d" else (kind, index, plane)] = t

    def of(index, kind, plane, up):
        t = numbers[(kind, plane) if kind == "d" else (kind, index, plane)]
        return message(D if kind == "d" else V.at[BASES[index]], plane, up, t)

    def send_round(index):
        for which, kind, plane in order:
            if which == index:

                @pl.when(has_below)
                def _(kind=kind, plane=plane):
                    of(index, kind, plane, False).start()

                @pl.when(has_above)
                def _(kind=kind, plane=plane):
                    of(index, kind, plane, True).start()

    def receive(index, kind, plane):
        @pl.when(has_below)
        def _():
            of(index, kind, plane, True).wait_recv()

        @pl.when(has_above)
        def _():
            of(index, kind, plane, False).wait_recv()

    lane = lax.broadcasted_iota(jnp.int32, (8, 128), 1)
    leftmost, rightmost = lane == 0, lane == 127
    scale = np.float32(2.0 / HALF)

    def scale_diag(first, count):
        def one(i, _):
            for c in range(chunks):
                at = pl.ds(PAD + 8 * c, 8)
                D[first + i, at, :] = (D[first + i, at, :] + np.float32(6.0 - MID)) * scale
            return 0

        lax.fori_loop(0, count, one, 0)

    def step(source, target, before, plane, keep=None):
        for c in range(chunks):
            at = pl.ds(PAD + 8 * c, 8)
            v = V[source, plane, at, :]
            sides = (V[source, plane - 1, at, :] + V[source, plane + 1, at, :]) + (
                V[source, plane, pl.ds(PAD + 8 * c - 1, 8), :]
                + V[source, plane, pl.ds(PAD + 8 * c + 1, 8), :]
            )
            sides = sides + (
                jnp.where(leftmost, 0.0, pltpu.roll(v, 1, 1))
                + jnp.where(rightmost, 0.0, pltpu.roll(v, 127, 1))
            )
            new = D[plane, at, :] * v - scale * sides
            new = 0.5 * new if before is None else new - V[before, plane, at, :]
            V[target, plane, at, :] = new if keep is None else jnp.where(keep, new, 0.0)

    def inner(base, steps):
        for j in range(1, steps + 1):
            before = None if j == 1 else base + j - 2

            def pair(i, _, j=j, before=before):
                first = GHOST + j + 2 * i
                step(base + j - 1, base + j, before, first)
                step(base + j - 1, base + j, before, first + 1)
                return 0

            lax.fori_loop(0, (planes - 2 * j) // 2, pair, 0)

    def wave(base, steps, g):
        low, high = GHOST - g, GHOST + planes - 1 + g

        def one(j, before):
            keep_low = jnp.logical_or(has_below, j >= g)
            keep_high = jnp.logical_or(has_above, j >= g)
            step(base + j - 1, base + j, before, low + j, keep_low)
            step(base + j - 1, base + j, before, high - j, keep_high)

        one(1, None)

        def later(j, _):
            one(j, base + j - 2)
            return 0

        lax.fori_loop(2, steps + 1, later, 0)

    pairs = [(i, j) for j in range(STEPS + 1) for i in range(j + 1)]
    place = {pair: i for i, pair in enumerate(pairs)}

    def products(first, last, two, slot):
        mine = [p for p in pairs if first <= p[1] <= last and p != (STEPS, STEPS)]

        def add(plane):
            def some(c, acc):
                acc = list(acc)
                for u in range(2):
                    at = pl.ds(pl.multiple_of(PAD + 16 * c + 8 * u, 8), 8)
                    v = [V[k, plane, at, :] for k in range(last + 1)]
                    for a, (i, j) in enumerate(mine):
                        acc[a] = acc[a] + v[i] * v[j]
                return tuple(acc)

            return some

        acc = tuple(zero for _ in mine)
        for plane in two:
            acc = lax.fori_loop(0, chunks // 2, add(plane), acc)
        for value, pair in zip(acc, mine):
            ACC[place[pair], slot] = value

    def all_products(first, last):
        def one(slot, _):
            products(first, last, (GHOST + 2 * slot, GHOST + 2 * slot + 1), slot)
            return 0

        lax.fori_loop(0, planes // 2, one, 0)

    def reduce(where, count):
        for pair, lanes in where.items():
            value = (ACC[place[pair], 0], zero)
            for slot in range(1, SLOTS):
                s, e = two_sum(value[0], ACC[place[pair], slot])
                value = (s, value[1] + e)
            for n in lanes:
                RED[0, 8 * n : 8 * n + 8, :] = value[0]
                RED[1, 8 * n : 8 * n + 8, :] = value[1]
        for q in range(16):
            if 8 * q >= count:
                PACK[0, 8 * q : 8 * q + 8, :] = zero
                PACK[1, 8 * q : 8 * q + 8, :] = zero
                continue
            total = tree2(
                [
                    tuple(RED[h, pl.ds(64 * q + s, 8, stride=8), :] for h in range(2))
                    for s in range(8)
                ]
            )
            PACK[0, 8 * q : 8 * q + 8, :] = total[0]
            PACK[1, 8 * q : 8 * q + 8, :] = total[1]
        high, low = jnp.transpose(PACK[0]), jnp.transpose(PACK[1])
        total = sublanes2(
            tree2([(high[8 * q : 8 * q + 8], low[8 * q : 8 * q + 8]) for q in range(16)])
        )
        return total

    def spread(k, o):
        return pltpu.make_async_remote_copy(
            src_ref=SEND.at[k],
            dst_ref=GOT.at[k, me],
            send_sem=all_send.at[k, o],
            recv_sem=all_recv.at[k, me],
            device_id={"slab": lax.rem(me + o, devices)},
            device_id_type=MESH,
        )

    def arrival(k, o):
        source = lax.rem(me + o, devices)
        return pltpu.make_async_remote_copy(
            src_ref=SEND.at[k],
            dst_ref=GOT.at[k, source],
            send_sem=all_send.at[k, o],
            recv_sem=all_recv.at[k, source],
            device_id={"slab": source},
            device_id_type=MESH,
        )

    def share(k, total):
        SEND[k, 0:1, :] = total[0][0:1]
        SEND[k, 1:2, :] = total[1][0:1]
        GOT[k, me, 0:1, :] = total[0][0:1]
        GOT[k, me, 1:2, :] = total[1][0:1]
        for o in range(1, devices):
            spread(k, o).start()

    def collect(k):
        for o in range(1, devices):
            arrival(k, o).wait_recv()
        value = (GOT[k, 0], jnp.zeros((2, 128), jnp.float32))
        for d in range(1, devices):
            s, e = two_sum(value[0], GOT[k, d])
            value = (s, value[1] + e)
        high = jnp.broadcast_to(value[0][0:1], (8, 128))
        low = jnp.broadcast_to(value[1][0:1] + value[0][1:2], (8, 128))
        return quick(high, low)

    for copy in loads[:4]:
        copy.wait()
    scale_diag(GHOST, deep)
    scale_diag(GHOST + planes - deep, deep)
    pl.semaphore_wait(barrier, devices - 1)
    send_round(0)
    for copy in loads[4:]:
        copy.wait()
    scale_diag(GHOST + deep, planes - 2 * deep)

    n = STEPS
    last_base, last_steps = BASES[-1], BLOCKS[-1]
    for index, (base, steps) in enumerate(zip(BASES, BLOCKS)):
        final = index + 1 == len(BLOCKS)
        if index > 0:
            send_round(index)
            all_products(BASES[index - 1] + 1 if index > 1 else 0, base)
        inner(base, steps)
        if final:

            def early(slot, _):
                at = GHOST + last_steps - 1 + 2 * slot
                products(base + 1, n - 1, (at, at + 1), slot)
                return 0

            def late(slot, _):
                at = GHOST + last_steps + 2 * slot
                products(n, n, (at, at + 1), slot)
                return 0

            lax.fori_loop(0, planes // 2 - last_steps + 1, early, 0)
            lax.fori_loop(0, planes // 2 - last_steps, late, 0)
        for g in range(1, steps + 1):
            receive(index, "v", g - 1)
            if g > 1 and ("d", g - 2) in numbers:
                which = order[numbers[("d", g - 2)]][0]
                if which == index or (index > 0 and which == index - 1 and g - 1 >= BLOCKS[index - 1]):
                    receive(which, "d", g - 2)
            wave(base, steps, g)
            if final:
                if g < steps:
                    near = steps - 1 - g
                    products(
                        base + 1,
                        n - 1,
                        (GHOST + near, GHOST + planes - 1 - near),
                        planes // 2 - steps + g,
                    )
                near = steps - g
                products(n, n, (GHOST + near, GHOST + planes - 1 - near), planes // 2 - steps + g - 1)
                if g == steps - 1:
                    where = {
                        (i, j): sorted({n * i + j, n * j + i}) for i, j in pairs if j < n
                    }
                    share(0, reduce(where, n * n))
    share(1, reduce({(i, n): [i] for i in range(n)}, n))

    table_load.wait()
    sub = lax.broadcasted_iota(jnp.int32, (8, 128), 0)
    got = collect(0)
    parts = []
    for h in range(2):
        top, bottom = zero, zero
        for i in range(n):
            moved = got[h] if i == 0 else pltpu.roll(got[h], 128 - n * i, 1)
            if i < 8:
                top = jnp.where(sub == i, moved, top)
            else:
                bottom = jnp.where(sub == i - 8, moved, bottom)
        both = jnp.concatenate([top, bottom], axis=0)
        wide = lax.broadcasted_iota(jnp.int32, (16, 128), 1)
        parts.append(jnp.where(wide < n, both, TAB[h, 0:16, :]))
    M = tuple(parts)
    row = lax.broadcasted_iota(jnp.int32, (16, 128), 0)
    for k in range(n):
        column = tuple(jnp.broadcast_to(m[:, k : k + 1], (16, 128)) for m in M)
        pivot = tuple(jnp.broadcast_to(c[k : k + 1, :], (16, 128)) for c in column)
        scaled = mul2(tuple(jnp.broadcast_to(m[k : k + 1, :], (16, 128)) for m in M), inverse2(pivot))
        rest = add2(M, neg2(mul2(column, scaled)))
        M = tuple(jnp.where(row == k, s, m) for s, m in zip(scaled, rest))
    got = collect(1)
    wide = lax.broadcasted_iota(jnp.int32, (16, 128), 1)
    H = tuple(
        jnp.broadcast_to(
            jnp.sum(
                jnp.where(wide == row, jnp.concatenate([v, v], axis=0), 0.0), axis=1, keepdims=True
            ),
            (16, 128),
        )
        for v in got
    )
    H = tuple(jnp.where(row < n, v, 0.0) for v in H)
    M = tuple(jnp.where(row < n, m, 0.0) for m in M)
    terms = mul2(M, H)
    terms = sublanes2(add2(tuple(t[0:8] for t in terms), tuple(t[8:16] for t in terms)))
    terms = add2(terms, (TAB[0, 16:24, :], TAB[1, 16:24, :]))
    value = tuple(
        jnp.broadcast_to(t[:, SHIFT + 2 * n + 1 : SHIFT + 2 * n + 2], (8, 128)) for t in terms
    )
    terms = mul2(terms, inverse2(value))
    factor = terms[0]
    fx = [jnp.broadcast_to(factor[:, SHIFT + i : SHIFT + i + 1], (8, 128)) for i in range(n)]
    fr = [
        jnp.broadcast_to(factor[:, SHIFT + n + i : SHIFT + n + i + 1], (8, 128))
        for i in range(n + 1)
    ]

    for index, kind, plane in order:

        @pl.when(has_below)
        def _(index=index, kind=kind, plane=plane):
            of(index, kind, plane, False).wait_send()

        @pl.when(has_above)
        def _(index=index, kind=kind, plane=plane):
            of(index, kind, plane, True).wait_send()

    stores = []
    group = 4
    for q in range(planes // group):

        def one(i, _, q=q):
            plane = GHOST + group * q + i
            for c in range(chunks):
                at = pl.ds(PAD + 8 * c, 8)
                v = [V[k, plane, at, :] for k in range(n + 1)]
                V[0, plane, at, :] = functools.reduce(jnp.add, [f * u for f, u in zip(fx, v)])
                V[1, plane, at, :] = functools.reduce(jnp.add, [f * u for f, u in zip(fr, v)])
            return 0

        lax.fori_loop(0, group, one, 0)
        for k, out in enumerate((x_ref, r_ref)):
            copy = pltpu.make_async_copy(
                V.at[k, pl.ds(GHOST + group * q, group), body],
                out.at[pl.ds(group * q, group)],
                store_sem.at[k, q],
            )
            copy.start()
            stores.append(copy)

    for k in range(2):
        for o in range(1, devices):
            spread(k, o).wait_send()
    for copy in stores:
        copy.wait()


def local(right_side, diagonal):
    planes, rows, lanes = right_side.shape
    devices = lax.axis_size("slab")
    count = 64
    tall = planes + 2 * GHOST
    f32 = jnp.float32
    out = jax.ShapeDtypeStruct(right_side.shape, f32)
    dma = pltpu.SemaphoreType.DMA
    return pl.pallas_call(
        functools.partial(kernel, devices),
        out_shape=(out, out),
        in_specs=[pl.BlockSpec(memory_space=pl.ANY)] * 3,
        out_specs=(pl.BlockSpec(memory_space=pl.ANY),) * 2,
        scratch_shapes=[
            pltpu.VMEM((STEPS + 1, tall, rows + 2 * PAD, lanes), f32),
            pltpu.VMEM((tall, rows + 2 * PAD, lanes), f32),
            pltpu.VMEM(((STEPS + 1) * (STEPS + 2) // 2, SLOTS, 8, 128), f32),
            pltpu.VMEM((2, 1024, 128), f32),
            pltpu.VMEM((2, 128, 128), f32),
            pltpu.VMEM((2, 2, 128), f32),
            pltpu.VMEM((2, devices, 2, 128), f32),
            pltpu.VMEM((2, 24, 128), f32),
            dma((7,)),
            dma((2, count)),
            dma((2, count)),
            dma((2, devices)),
            dma((2, devices)),
            dma((2, planes // 4)),
        ],
        compiler_params=pltpu.CompilerParams(collective_id=0, has_side_effects=True),
        name="cg",
    )(right_side, diagonal, jnp.asarray(tables()))


def solution(mesh):
    placed = (P("slab", "sys", None), P("slab", "sys", None))
    return jax.shard_map(
        local,
        mesh=mesh,
        in_specs=placed,
        out_specs=placed,
        check_vma=False,
    )
```

time: 323 us -> 62.7 us (0.19)
  starting transfers between devices: 129 us -> 0 us
  other arithmetic: 81 us -> 0 us
  Pallas kernels: 0 us -> 58.6 us
  local copies, waits for them, and re-layouts: 44.7 us -> 3.36 us
  between operations: 37.5 us -> 0.65 us
  waiting for transfers between devices: 14.8 us -> 0 us
  blocking collectives: 14.7 us -> 0 us
    all_to_all x9 -> x0, starting transfers between devices: 69.8 us -> none  [copy_for_each(): return lax.all_to_all(copies, axis, split_axis=0, concat_axis=0, tiled=True)]
    reduce_sum x20 -> x0, other arithmetic: 60.6 us -> none  [the longest x10 60.3 us: paired_sums(): jnp.sum(residual * residual)]
    ppermute x20 -> x0, starting transfers between devices: 58.7 us -> none  [the longest x10 45.8 us: with_halo(): lax.ppermute(tail, axis, [(i, (i + 1) % count) for i in range(ends)])]
    pallas_call x0 -> x1, Pallas kernels: none -> 58.6 us  [local(): pl.pallas_call(functools.partial(kernel, devices), out_shape=(out, out),...]
    slice x40 -> x0, local copies, waits for them, and re-layouts: 38.2 us -> none  [the longest x10 16.9 us: operate(): beside = beside + jnp.pad(values[:, :, 1:], ((0, 0), (0, 0), (0, 1)))]
    all_to_all x9 -> x0, waiting for transfers between devices: 14.8 us -> none  [copy_for_each(): return lax.all_to_all(copies, axis, split_axis=0, concat_axis=0, tiled=True)]
    all_to_all x1 -> x0, blocking collectives: 14.7 us -> none  [copy_for_each(): return lax.all_to_all(copies, axis, split_axis=0, concat_axis=0, tiled=True)]
    concatenate x10 -> x0, other arithmetic: 13 us -> none  [together(): line, at, outs = (jnp.concatenate([a.reshape(-1) for a in arrays]), 0, [])]
  transfers between devices with their start and end apart: 29 -> 0, of which waited for: 9 -> 0; matrix products, arithmetic and copies ran while one was open for 2% -> 0% of each run, Pallas kernels for 0% -> 0%
where the time goes in v1:
time: 62.7 us; the launch traced here: 62.6 us
  Pallas kernels  58.6 us (93%)
  local copies, waits for them, and re-layouts  3.36 us (5%)
  between operations  0.65 us (1%)
    pallas_call x1, Pallas kernels, local(): pl.pallas_call(functools.partial(kernel, devices), out_shape=(out, out),...  58.6 us
    unnamed x4, local copies, waits for them, and re-layouts  3.36 us

profile of v1, /device:TPU:0, one launch (start us, length us, event | category | flops | bytes accessed | tf_op | source)
XLA Modules:
  0.0 62.6 jit_solution(13931853595575594861)
XLA Ops:
  0.6 58.6 %cg.1 = (f32[16,128,128]{2,1,0:T(8,128)}, f32[16,128,128]{2,1,0:T(8,128)}) custom-call(f32[16,128,128]{2,1,0:T(8,128)} %right_ref.1, f32[16,128,128]{2,1,0:T(8,128)} %diag_ref.1, f32[2,24,128]{2,1,0:T(8,128)} %constant.2.clone.table_ref), custom_call_target="tpu_custom_call" | custom-call | tf_op jit(solution)/shard_map/cg/pallas_call | solution.py:547
  59.2 0.0 copy-start
  59.2 2.4 %copy.7 = f32[16,128,128]{2,1,0:T(8,128)} copy(f32[16,128,128]{2,1,0:T(8,128)} %get-tuple-element.4) | data formatting | bytes 2097152
  61.6 0.0 copy-done
  61.6 1.0 %copy.8 = f32[16,128,128]{2,1,0:T(8,128)} copy(f32[16,128,128]{2,1,0:T(8,128)S(1)} %copy-done) | data formatting | bytes 2097152
Async XLA Ops:
  59.2 2.4 %copy-start = (f32[16,128,128]{2,1,0:T(8,128)S(1)}, f32[16,128,128]{2,1,0:T(8,128)}, u32[]{:S(2)}) copy-start(f32[16,128,128]{2,1,0:T(8,128)} %get-tuple-element.5) | copy-start | bytes 3145732

commit v2 on v1

--- a/solution.py
+++ b/solution.py
@@ -120,7 +120,6 @@
     recv_sem,
     all_send,
     all_recv,
-    store_sem,
 ):
     planes, rows = right_ref.shape[0], right_ref.shape[1]
     chunks = rows // 8
@@ -277,18 +276,12 @@
         low, high = GHOST - g, GHOST + planes - 1 + g
 
         def one(j, before):
-            keep_low = jnp.logical_or(has_below, j >= g)
-            keep_high = jnp.logical_or(has_above, j >= g)
+            keep_low, keep_high = (None, None) if j >= g else (has_below, has_above)
             step(base + j - 1, base + j, before, low + j, keep_low)
             step(base + j - 1, base + j, before, high - j, keep_high)
 
-        one(1, None)
-
-        def later(j, _):
-            one(j, base + j - 2)
-            return 0
-
-        lax.fori_loop(2, steps + 1, later, 0)
+        for j in range(1, steps + 1):
+            one(j, None if j == 1 else base + j - 2)
 
     pairs = [(i, j) for j in range(STEPS + 1) for i in range(j + 1)]
     place = {pair: i for i, pair in enumerate(pairs)}
@@ -299,8 +292,8 @@
         def add(plane):
             def some(c, acc):
                 acc = list(acc)
-                for u in range(2):
-                    at = pl.ds(pl.multiple_of(PAD + 16 * c + 8 * u, 8), 8)
+                for u in range(4):
+                    at = pl.ds(pl.multiple_of(PAD + 32 * c + 8 * u, 8), 8)
                     v = [V[k, plane, at, :] for k in range(last + 1)]
                     for a, (i, j) in enumerate(mine):
                         acc[a] = acc[a] + v[i] * v[j]
@@ -310,7 +303,7 @@
 
         acc = tuple(zero for _ in mine)
         for plane in two:
-            acc = lax.fori_loop(0, chunks // 2, add(plane), acc)
+            acc = lax.fori_loop(0, chunks // 4, add(plane), acc)
         for value, pair in zip(acc, mine):
             ACC[place[pair], slot] = value
 
@@ -445,6 +438,19 @@
                     }
                     share(0, reduce(where, n * n))
     share(1, reduce({(i, n): [i] for i in range(n)}, n))
+    for index, kind, plane in order:
+
+        @pl.when(has_below)
+        def _(index=index, kind=kind, plane=plane):
+            of(index, kind, plane, False).wait_send()
+
+        @pl.when(has_above)
+        def _(index=index, kind=kind, plane=plane):
+            of(index, kind, plane, True).wait_send()
+
+    for k in range(2):
+        for o in range(1, devices):
+            spread(k, o).wait_send()
 
     table_load.wait()
     sub = lax.broadcasted_iota(jnp.int32, (8, 128), 0)
@@ -496,43 +502,27 @@
         for i in range(n + 1)
     ]
 
-    for index, kind, plane in order:
-
-        @pl.when(has_below)
-        def _(index=index, kind=kind, plane=plane):
-            of(index, kind, plane, False).wait_send()
-
-        @pl.when(has_above)
-        def _(index=index, kind=kind, plane=plane):
-            of(index, kind, plane, True).wait_send()
-
-    stores = []
-    group = 4
-    for q in range(planes // group):
-
-        def one(i, _, q=q):
-            plane = GHOST + group * q + i
-            for c in range(chunks):
-                at = pl.ds(PAD + 8 * c, 8)
-                v = [V[k, plane, at, :] for k in range(n + 1)]
-                V[0, plane, at, :] = functools.reduce(jnp.add, [f * u for f, u in zip(fx, v)])
-                V[1, plane, at, :] = functools.reduce(jnp.add, [f * u for f, u in zip(fr, v)])
-            return 0
-
-        lax.fori_loop(0, group, one, 0)
-        for k, out in enumerate((x_ref, r_ref)):
-            copy = pltpu.make_async_copy(
-                V.at[k, pl.ds(GHOST + group * q, group), body],
-                out.at[pl.ds(group * q, group)],
-                store_sem.at[k, q],
-            )
-            copy.start()
-            stores.append(copy)
-
-    for k in range(2):
-        for o in range(1, devices):
-            spread(k, o).wait_send()
-    for copy in stores:
+    def one(i, _):
+        plane = GHOST + i
+        for c in range(chunks):
+            at = pl.ds(PAD + 8 * c, 8)
+            v = [V[k, plane, at, :] for k in range(n + 1)]
+            x_ref[i, 8 * c : 8 * c + 8, :] = functools.reduce(jnp.add, [f * u for f, u in zip(fx, v)])
+            r_ref[i, 8 * c : 8 * c + 8, :] = functools.reduce(jnp.add, [f * u for f, u in zip(fr, v)])
+        return 0
+
+    lax.fori_loop(0, planes, one, 0)
+
+
+def store_kernel(x_ref, r_ref, x_out, r_out, sem):
+    group = x_ref.shape[0] // 4
+    copies = []
+    for q in range(4):
+        for k, (source, target) in enumerate(((x_ref, x_out), (r_ref, r_out))):
+            at = pl.ds(group * q, group)
+            copies.append(pltpu.make_async_copy(source.at[at], target.at[at], sem.at[k, q]))
+            copies[-1].start()
+    for copy in copies:
         copy.wait()
 
 
@@ -543,12 +533,13 @@
     tall = planes + 2 * GHOST
     f32 = jnp.float32
     out = jax.ShapeDtypeStruct(right_side.shape, f32)
+    held = pltpu.VMEM(right_side.shape, f32)
     dma = pltpu.SemaphoreType.DMA
-    return pl.pallas_call(
+    results = pl.pallas_call(
         functools.partial(kernel, devices),
-        out_shape=(out, out),
-        in_specs=[pl.BlockSpec(memory_space=pl.ANY)] * 3,
-        out_specs=(pl.BlockSpec(memory_space=pl.ANY),) * 2,
+        out_shape=(held, held),
+        in_specs=[pl.BlockSpec(memory_space=pltpu.HBM)] * 3,
+        out_specs=(pl.BlockSpec(memory_space=pltpu.VMEM),) * 2,
         scratch_shapes=[
             pltpu.VMEM((STEPS + 1, tall, rows + 2 * PAD, lanes), f32),
             pltpu.VMEM((tall, rows + 2 * PAD, lanes), f32),
@@ -563,11 +554,25 @@
             dma((2, count)),
             dma((2, devices)),
             dma((2, devices)),
-            dma((2, planes // 4)),
         ],
-        compiler_params=pltpu.CompilerParams(collective_id=0, has_side_effects=True),
+        compiler_params=pltpu.CompilerParams(
+            collective_id=0, has_side_effects=True, vmem_limit_bytes=40 * 2**20
+        ),
         name="cg",
-    )(right_side, diagonal, jnp.asarray(tables()))
+    )(
+        *(
+            pltpu.with_memory_space_constraint(a, pltpu.HBM)
+            for a in (right_side, diagonal, jnp.asarray(tables()))
+        )
+    )
+    return pl.pallas_call(
+        store_kernel,
+        out_shape=(out, out),
+        in_specs=[pl.BlockSpec(memory_space=pltpu.VMEM)] * 2,
+        out_specs=(pl.BlockSpec(memory_space=pltpu.HBM),) * 2,
+        scratch_shapes=[dma((2, 4))],
+        name="store",
+    )(*(pltpu.with_memory_space_constraint(a, pltpu.VMEM) for a in results))
 
 
 def solution(mesh):

time: 62.7 us -> 46.1 us (0.74)
  Pallas kernels: 58.6 us -> 45.4 us
  local copies, waits for them, and re-layouts: 3.36 us -> 0 us
    pallas_call x1 -> x2, Pallas kernels: 58.6 us -> 45.4 us  [the longest x1 44 us: local(): pl.pallas_call(functools.partial(kernel, devices), out_shape=(held, held)...]
    unnamed x4 -> x0, local copies, waits for them, and re-layouts: 3.36 us -> none
where the time goes in v2:
time: 46.1 us; the launch traced here: 46 us
  Pallas kernels  45.4 us (98%)
  between operations  0.64 us (1%)
    pallas_call x1, Pallas kernels, local(): pl.pallas_call(functools.partial(kernel, devices), out_shape=(held, held)...  44 us
    pallas_call x1, Pallas kernels, local(): pl.pallas_call(store_kernel, out_shape=(out, out), in_specs=[pl.BlockSpec...  1.38 us

profile of v2, /device:TPU:0, one launch (start us, length us, event | category | flops | bytes accessed | tf_op | source)
XLA Modules:
  0.0 46.0 jit_solution(16649701318567813357)
XLA Ops:
  0.6 44.0 %cg.1 = (f32[16,128,128]{2,1,0:T(8,128)S(1)}, f32[16,128,128]{2,1,0:T(8,128)S(1)}) custom-call(f32[16,128,128]{2,1,0:T(8,128)} %right_ref.1, f32[16,128,128]{2,1,0:T(8,128)} %diag_ref.1, f32[2,24,128]{2,1,0:T(8,128)} %constant.2.clone.table_ref), custom_call_target="tpu_custom_call" | custom-call | tf_op jit(solution)/shard_map/cg/pallas_call | solution.py:538
  44.6 1.4 %store.1 = (f32[16,128,128]{2,1,0:T(8,128)}, f32[16,128,128]{2,1,0:T(8,128)}) custom-call(f32[16,128,128]{2,1,0:T(8,128)S(1)} %get-tuple-element.4.x_ref, f32[16,128,128]{2,1,0:T(8,128)S(1)} %get-tuple-element.5.r_ref), custom_call_target="tpu_custom_call" | custom-call | tf_op jit(solution)/shard_map/store/pallas_call | solution.py:568

commit v3 on v2

--- a/solution.py
+++ b/solution.py
@@ -14,6 +14,7 @@
 STEPS = sum(BLOCKS)
 BASES = tuple(int(b) for b in np.cumsum((0,) + BLOCKS[:-1]))
 GHOST = max(BLOCKS)
+MESSAGES = STEPS + GHOST - 1
 PAD = 8
 SLOTS = 8
 SHIFT = 32
@@ -185,7 +186,7 @@
         return pltpu.make_async_remote_copy(
             src_ref=array.at[source, body],
             dst_ref=array.at[target, body],
-            send_sem=send_sem.at[int(up), t],
+            send_sem=send_sem.at[int(up)],
             recv_sem=recv_sem.at[int(up), t],
             device_id={"slab": above if up else below},
             device_id_type=MESH,
@@ -210,17 +211,22 @@
         t = numbers[(kind, plane) if kind == "d" else (kind, index, plane)]
         return message(D if kind == "d" else V.at[BASES[index]], plane, up, t)
 
-    def send_round(index):
-        for which, kind, plane in order:
-            if which == index:
-
-                @pl.when(has_below)
-                def _(kind=kind, plane=plane):
-                    of(index, kind, plane, False).start()
-
-                @pl.when(has_above)
-                def _(kind=kind, plane=plane):
-                    of(index, kind, plane, True).start()
+    def send(index, kind, plane):
+        @pl.when(has_below)
+        def _():
+            of(index, kind, plane, False).start()
+
+        @pl.when(has_above)
+        def _():
+            of(index, kind, plane, True).start()
+
+    def wait_sent():
+        for up, there in ((False, has_below), (True, has_above)):
+
+            @pl.when(there)
+            def _(up=up):
+                sent = D.at[pl.ds(0, len(order)), body]
+                pltpu.make_async_copy(sent, sent, send_sem.at[int(up)]).wait()
 
     def receive(index, kind, plane):
         @pl.when(has_below)
@@ -307,12 +313,20 @@
         for value, pair in zip(acc, mine):
             ACC[place[pair], slot] = value
 
-    def all_products(first, last):
+    def inner_products(first, last, near):
         def one(slot, _):
-            products(first, last, (GHOST + 2 * slot, GHOST + 2 * slot + 1), slot)
+            at = GHOST + near + 2 * slot
+            products(first, last, (at, at + 1), slot)
             return 0
 
-        lax.fori_loop(0, planes // 2, one, 0)
+        lax.fori_loop(0, planes // 2 - near, one, 0)
+
+    def outer_products(first, last, near):
+        def one(i, _):
+            products(first, last, (GHOST + i, GHOST + planes - 1 - i), planes // 2 - near + i)
+            return 0
+
+        lax.fori_loop(0, near, one, 0)
 
     def reduce(where, count):
         for pair, lanes in where.items():
@@ -346,20 +360,9 @@
         return pltpu.make_async_remote_copy(
             src_ref=SEND.at[k],
             dst_ref=GOT.at[k, me],
-            send_sem=all_send.at[k, o],
-            recv_sem=all_recv.at[k, me],
+            send_sem=all_send.at[k],
+            recv_sem=all_recv.at[k],
             device_id={"slab": lax.rem(me + o, devices)},
-            device_id_type=MESH,
-        )
-
-    def arrival(k, o):
-        source = lax.rem(me + o, devices)
-        return pltpu.make_async_remote_copy(
-            src_ref=SEND.at[k],
-            dst_ref=GOT.at[k, source],
-            send_sem=all_send.at[k, o],
-            recv_sem=all_recv.at[k, source],
-            device_id={"slab": source},
             device_id_type=MESH,
         )
 
@@ -371,9 +374,17 @@
         for o in range(1, devices):
             spread(k, o).start()
 
+    def wait_shared():
+        for k in range(2):
+            sent = GOT.at[k, pl.ds(0, devices - 1)]
+            pltpu.make_async_copy(sent, sent, all_send.at[k]).wait()
+
+    def wait_row(k):
+        arrived = GOT.at[k, pl.ds(0, devices - 1)]
+        pltpu.make_async_copy(arrived, arrived, all_recv.at[k]).wait()
+
     def collect(k):
-        for o in range(1, devices):
-            arrival(k, o).wait_recv()
+        wait_row(k)
         value = (GOT[k, 0], jnp.zeros((2, 128), jnp.float32))
         for d in range(1, devices):
             s, e = two_sum(value[0], GOT[k, d])
@@ -384,36 +395,33 @@
 
     for copy in loads[:4]:
         copy.wait()
+    pl.semaphore_wait(barrier, devices - 1)
+    send(0, "v", 0)
     scale_diag(GHOST, deep)
     scale_diag(GHOST + planes - deep, deep)
-    pl.semaphore_wait(barrier, devices - 1)
-    send_round(0)
+    for which, kind, plane in order[1:]:
+        if which == 0:
+            send(0, kind, plane)
     for copy in loads[4:]:
         copy.wait()
     scale_diag(GHOST + deep, planes - 2 * deep)
 
     n = STEPS
-    last_base, last_steps = BASES[-1], BLOCKS[-1]
     for index, (base, steps) in enumerate(zip(BASES, BLOCKS)):
         final = index + 1 == len(BLOCKS)
-        if index > 0:
-            send_round(index)
-            all_products(BASES[index - 1] + 1 if index > 1 else 0, base)
+        after = 0 if final else BLOCKS[index + 1]
+        rows_from = base + 1 if index else 0
+        for which, kind, plane in order:
+            if index and which == index and kind == "d":
+                send(index, kind, plane)
         inner(base, steps)
+        for plane in range(steps, after):
+            send(index + 1, "v", plane)
+        if index:
+            outer_products(BASES[index - 1] + 1 if index > 1 else 0, base, BLOCKS[index - 1])
+        inner_products(rows_from, n - 1 if final else base + steps, steps - 1 if final else steps)
         if final:
-
-            def early(slot, _):
-                at = GHOST + last_steps - 1 + 2 * slot
-                products(base + 1, n - 1, (at, at + 1), slot)
-                return 0
-
-            def late(slot, _):
-                at = GHOST + last_steps + 2 * slot
-                products(n, n, (at, at + 1), slot)
-                return 0
-
-            lax.fori_loop(0, planes // 2 - last_steps + 1, early, 0)
-            lax.fori_loop(0, planes // 2 - last_steps, late, 0)
+            inner_products(n, n, steps)
         for g in range(1, steps + 1):
             receive(index, "v", g - 1)
             if g > 1 and ("d", g - 2) in numbers:
@@ -421,6 +429,8 @@
                 if which == index or (index > 0 and which == index - 1 and g - 1 >= BLOCKS[index - 1]):
                     receive(which, "d", g - 2)
             wave(base, steps, g)
+            if index == 0 and steps - g < after:
+                send(index + 1, "v", steps - g)
             if final:
                 if g < steps:
                     near = steps - 1 - g
@@ -437,20 +447,12 @@
                         (i, j): sorted({n * i + j, n * j + i}) for i, j in pairs if j < n
                     }
                     share(0, reduce(where, n * n))
+        if index:
+            for plane in range(min(steps, after)):
+                send(index + 1, "v", plane)
     share(1, reduce({(i, n): [i] for i in range(n)}, n))
-    for index, kind, plane in order:
-
-        @pl.when(has_below)
-        def _(index=index, kind=kind, plane=plane):
-            of(index, kind, plane, False).wait_send()
-
-        @pl.when(has_above)
-        def _(index=index, kind=kind, plane=plane):
-            of(index, kind, plane, True).wait_send()
-
-    for k in range(2):
-        for o in range(1, devices):
-            spread(k, o).wait_send()
+    wait_sent()
+    wait_shared()
 
     table_load.wait()
     sub = lax.broadcasted_iota(jnp.int32, (8, 128), 0)
@@ -529,7 +531,6 @@
 def local(right_side, diagonal):
     planes, rows, lanes = right_side.shape
     devices = lax.axis_size("slab")
-    count = 64
     tall = planes + 2 * GHOST
     f32 = jnp.float32
     out = jax.ShapeDtypeStruct(right_side.shape, f32)
@@ -550,10 +551,10 @@
             pltpu.VMEM((2, devices, 2, 128), f32),
             pltpu.VMEM((2, 24, 128), f32),
             dma((7,)),
-            dma((2, count)),
-            dma((2, count)),
-            dma((2, devices)),
-            dma((2, devices)),
+            dma((2,)),
+            dma((2, MESSAGES)),
+            dma((2,)),
+            dma((2,)),
         ],
         compiler_params=pltpu.CompilerParams(
             collective_id=0, has_side_effects=True, vmem_limit_bytes=40 * 2**20

time: 46.1 us -> 42 us (0.911)
  Pallas kernels: 45.4 us -> 41.2 us
    pallas_call x1, Pallas kernels: 44 us -> 39.9 us  [local(): pl.pallas_call(functools.partial(kernel, devices), out_shape=(held, held)...]
where the time goes in v3:
time: 42 us; the launch traced here: 41.9 us
  Pallas kernels  41.2 us (98%)
  between operations  0.64 us (2%)
    pallas_call x1, Pallas kernels, local(): pl.pallas_call(functools.partial(kernel, devices), out_shape=(held, held)...  39.9 us
    pallas_call x1, Pallas kernels, local(): pl.pallas_call(store_kernel, out_shape=(out, out), in_specs=[pl.BlockSpec...  1.38 us

profile of v3, /device:TPU:0, one launch (start us, length us, event | category | flops | bytes accessed | tf_op | source)
XLA Modules:
  0.0 41.9 jit_solution(1556373975244017579)
XLA Ops:
  0.6 39.9 %cg.1 = (f32[16,128,128]{2,1,0:T(8,128)S(1)}, f32[16,128,128]{2,1,0:T(8,128)S(1)}) custom-call(f32[16,128,128]{2,1,0:T(8,128)} %right_ref.1, f32[16,128,128]{2,1,0:T(8,128)} %diag_ref.1, f32[2,24,128]{2,1,0:T(8,128)} %constant.2.clone.table_ref), custom_call_target="tpu_custom_call" | custom-call | tf_op jit(solution)/shard_map/cg/pallas_call | solution.py:539
  40.5 1.4 %store.1 = (f32[16,128,128]{2,1,0:T(8,128)}, f32[16,128,128]{2,1,0:T(8,128)}) custom-call(f32[16,128,128]{2,1,0:T(8,128)S(1)} %get-tuple-element.4.x_ref, f32[16,128,128]{2,1,0:T(8,128)S(1)} %get-tuple-element.5.r_ref), custom_call_target="tpu_custom_call" | custom-call | tf_op jit(solution)/shard_map/store/pallas_call | solution.py:569

commit v4 on v3

--- a/solution.py
+++ b/solution.py
@@ -106,9 +106,8 @@
     right_ref,
     diag_ref,
     table_ref,
-    x_ref,
-    r_ref,
     V,
+    COEF,
     D,
     ACC,
     RED,
@@ -266,17 +265,24 @@
             new = 0.5 * new if before is None else new - V[before, plane, at, :]
             V[target, plane, at, :] = new if keep is None else jnp.where(keep, new, 0.0)
 
-    def inner(base, steps):
+    def inner(base, steps, near):
         for j in range(1, steps + 1):
             before = None if j == 1 else base + j - 2
 
             def pair(i, _, j=j, before=before):
-                first = GHOST + j + 2 * i
+                first = GHOST + near + j + 2 * i
                 step(base + j - 1, base + j, before, first)
                 step(base + j - 1, base + j, before, first + 1)
                 return 0
 
-            lax.fori_loop(0, (planes - 2 * j) // 2, pair, 0)
+            lax.fori_loop(0, planes // 2 - near - j, pair, 0)
+
+    def inner_rest(base, steps, near):
+        for j in range(1, steps + 1):
+            before = None if j == 1 else base + j - 2
+            for i in range(j, j + near):
+                step(base + j - 1, base + j, before, GHOST + i)
+                step(base + j - 1, base + j, before, GHOST + planes - 1 - i)
 
     def wave(base, steps, g):
         low, high = GHOST - g, GHOST + planes - 1 + g
@@ -313,7 +319,7 @@
         for value, pair in zip(acc, mine):
             ACC[place[pair], slot] = value
 
-    def inner_products(first, last, near):
+    def middle_products(first, last, near):
         def one(slot, _):
             at = GHOST + near + 2 * slot
             products(first, last, (at, at + 1), slot)
@@ -321,12 +327,12 @@
 
         lax.fori_loop(0, planes // 2 - near, one, 0)
 
-    def outer_products(first, last, near):
+    def side_products(first, last, start, stop):
         def one(i, _):
-            products(first, last, (GHOST + i, GHOST + planes - 1 - i), planes // 2 - near + i)
+            products(first, last, (GHOST + i, GHOST + planes - 1 - i), planes // 2 - 1 - i)
             return 0
 
-        lax.fori_loop(0, near, one, 0)
+        lax.fori_loop(start, stop, one, 0)
 
     def reduce(where, count):
         for pair, lanes in where.items():
@@ -407,21 +413,35 @@
     scale_diag(GHOST + deep, planes - 2 * deep)
 
     n = STEPS
+
+    def begin(index):
+        base, steps, near = BASES[index], BLOCKS[index], BLOCKS[index - 1] if index else 0
+        final = index + 1 == len(BLOCKS)
+        inner(base, steps, near)
+        last = n - 1 if final else base + steps
+        middle_products(base + 1 if index else 0, last, near + steps - final)
+        if final:
+            middle_products(n, n, near + steps)
+
+    begin(0)
     for index, (base, steps) in enumerate(zip(BASES, BLOCKS)):
         final = index + 1 == len(BLOCKS)
         after = 0 if final else BLOCKS[index + 1]
-        rows_from = base + 1 if index else 0
-        for which, kind, plane in order:
-            if index and which == index and kind == "d":
-                send(index, kind, plane)
-        inner(base, steps)
-        for plane in range(steps, after):
-            send(index + 1, "v", plane)
         if index:
-            outer_products(BASES[index - 1] + 1 if index > 1 else 0, base, BLOCKS[index - 1])
-        inner_products(rows_from, n - 1 if final else base + steps, steps - 1 if final else steps)
-        if final:
-            inner_products(n, n, steps)
+            near = BLOCKS[index - 1]
+            for which, kind, plane in order:
+                if which == index and kind == "d":
+                    send(index, kind, plane)
+            inner_rest(base, steps, near)
+            for plane in range(steps, after):
+                send(index + 1, "v", plane)
+            side_products(BASES[index - 1] + 1 if index > 1 else 0, base, 0, near)
+            if final:
+                side_products(base + 1, n - 1, steps - 1, steps - 1 + near)
+                side_products(n, n, steps, steps + near)
+            else:
+                side_products(base + 1, base + steps, steps, steps + near)
+                begin(index + 1)
         for g in range(1, steps + 1):
             receive(index, "v", g - 1)
             if g > 1 and ("d", g - 2) in numbers:
@@ -429,8 +449,13 @@
                 if which == index or (index > 0 and which == index - 1 and g - 1 >= BLOCKS[index - 1]):
                     receive(which, "d", g - 2)
             wave(base, steps, g)
-            if index == 0 and steps - g < after:
-                send(index + 1, "v", steps - g)
+            if index == 0:
+                if steps - g < after:
+                    send(1, "v", steps - g)
+                if g == 1:
+                    for plane in range(steps, after):
+                        send(1, "v", plane)
+                    begin(1)
             if final:
                 if g < steps:
                     near = steps - 1 - g
@@ -438,10 +463,10 @@
                         base + 1,
                         n - 1,
                         (GHOST + near, GHOST + planes - 1 - near),
-                        planes // 2 - steps + g,
+                        planes // 2 - 1 - near,
                     )
                 near = steps - g
-                products(n, n, (GHOST + near, GHOST + planes - 1 - near), planes // 2 - steps + g - 1)
+                products(n, n, (GHOST + near, GHOST + planes - 1 - near), planes // 2 - 1 - near)
                 if g == steps - 1:
                     where = {
                         (i, j): sorted({n * i + j, n * j + i}) for i, j in pairs if j < n
@@ -498,30 +523,30 @@
     )
     terms = mul2(terms, inverse2(value))
     factor = terms[0]
-    fx = [jnp.broadcast_to(factor[:, SHIFT + i : SHIFT + i + 1], (8, 128)) for i in range(n)]
-    fr = [
-        jnp.broadcast_to(factor[:, SHIFT + n + i : SHIFT + n + i + 1], (8, 128))
-        for i in range(n + 1)
-    ]
+    for i in range(2 * n + 1):
+        COEF[i] = jnp.broadcast_to(factor[:, SHIFT + i : SHIFT + i + 1], (8, 128))
+
+
+def combine_kernel(V, COEF, x_out, r_out, X, R, sem):
+    planes, rows = X.shape[0], X.shape[1]
+    n = STEPS
+    fx = [COEF[i] for i in range(n)]
+    fr = [COEF[n + i] for i in range(n + 1)]
 
     def one(i, _):
-        plane = GHOST + i
-        for c in range(chunks):
-            at = pl.ds(PAD + 8 * c, 8)
-            v = [V[k, plane, at, :] for k in range(n + 1)]
-            x_ref[i, 8 * c : 8 * c + 8, :] = functools.reduce(jnp.add, [f * u for f, u in zip(fx, v)])
-            r_ref[i, 8 * c : 8 * c + 8, :] = functools.reduce(jnp.add, [f * u for f, u in zip(fr, v)])
+        for c in range(rows // 8):
+            at = pl.ds(8 * c, 8)
+            v = [V[k, GHOST + i, pl.ds(PAD + 8 * c, 8), :] for k in range(n + 1)]
+            X[i, at, :] = functools.reduce(jnp.add, [f * u for f, u in zip(fx, v)])
+            R[i, at, :] = functools.reduce(jnp.add, [f * u for f, u in zip(fr, v)])
         return 0
 
-    lax.fori_loop(0, planes, one, 0)
-
-
-def store_kernel(x_ref, r_ref, x_out, r_out, sem):
-    group = x_ref.shape[0] // 4
     copies = []
-    for q in range(4):
-        for k, (source, target) in enumerate(((x_ref, x_out), (r_ref, r_out))):
-            at = pl.ds(group * q, group)
+    group = 2
+    for q in range(planes // group):
+        lax.fori_loop(group * q, group * q + group, one, 0)
+        at = pl.ds(group * q, group)
+        for k, (source, target) in enumerate(((X, x_out), (R, r_out))):
             copies.append(pltpu.make_async_copy(source.at[at], target.at[at], sem.at[k, q]))
             copies[-1].start()
     for copy in copies:
@@ -534,15 +559,17 @@
     tall = planes + 2 * GHOST
     f32 = jnp.float32
     out = jax.ShapeDtypeStruct(right_side.shape, f32)
-    held = pltpu.VMEM(right_side.shape, f32)
+    held = (
+        pltpu.VMEM((STEPS + 1, tall, rows + 2 * PAD, lanes), f32),
+        pltpu.VMEM((2 * STEPS + 1, 8, 128), f32),
+    )
     dma = pltpu.SemaphoreType.DMA
     results = pl.pallas_call(
         functools.partial(kernel, devices),
-        out_shape=(held, held),
+        out_shape=held,
         in_specs=[pl.BlockSpec(memory_space=pltpu.HBM)] * 3,
         out_specs=(pl.BlockSpec(memory_space=pltpu.VMEM),) * 2,
         scratch_shapes=[
-            pltpu.VMEM((STEPS + 1, tall, rows + 2 * PAD, lanes), f32),
             pltpu.VMEM((tall, rows + 2 * PAD, lanes), f32),
             pltpu.VMEM(((STEPS + 1) * (STEPS + 2) // 2, SLOTS, 8, 128), f32),
             pltpu.VMEM((2, 1024, 128), f32),
@@ -557,7 +584,7 @@
             dma((2,)),
         ],
         compiler_params=pltpu.CompilerParams(
-            collective_id=0, has_side_effects=True, vmem_limit_bytes=40 * 2**20
+            collective_id=0, has_side_effects=True, vmem_limit_bytes=16 * 2**20
         ),
         name="cg",
     )(
@@ -567,12 +594,17 @@
         )
     )
     return pl.pallas_call(
-        store_kernel,
+        combine_kernel,
         out_shape=(out, out),
         in_specs=[pl.BlockSpec(memory_space=pltpu.VMEM)] * 2,
         out_specs=(pl.BlockSpec(memory_space=pltpu.HBM),) * 2,
-        scratch_shapes=[dma((2, 4))],
-        name="store",
+        scratch_shapes=[
+            pltpu.VMEM(right_side.shape, f32),
+            pltpu.VMEM(right_side.shape, f32),
+            dma((2, planes // 2)),
+        ],
+        compiler_params=pltpu.CompilerParams(vmem_limit_bytes=8 * 2**20),
+        name="combine",
     )(*(pltpu.with_memory_space_constraint(a, pltpu.VMEM) for a in results))
 
 

time: 42 us -> 39.7 us (0.945)
  Pallas kernels: 41.2 us -> 38.9 us
    pallas_call x2, Pallas kernels: 41.2 us -> 38.9 us  [the longest x1 36.6 us: local(): pl.pallas_call(functools.partial(kernel, devices), out_shape=held, in_spe...]
where the time goes in v4:
time: 39.7 us; the launch traced here: 39.6 us
  Pallas kernels  38.9 us (98%)
  between operations  0.64 us (2%)
    pallas_call x1, Pallas kernels, local(): pl.pallas_call(functools.partial(kernel, devices), out_shape=held, in_spe...  36.6 us
    pallas_call x1, Pallas kernels, local(): pl.pallas_call(combine_kernel, out_shape=(out, out), in_specs=[pl.BlockSp...  2.34 us

profile of v4, /device:TPU:0, one launch (start us, length us, event | category | flops | bytes accessed | tf_op | source)
XLA Modules:
  0.0 39.6 jit_solution(12868205517711628466)
XLA Ops:
  0.6 36.6 %cg.1 = (f32[11,24,144,128]{3,2,1,0:T(8,128)S(1)}, f32[21,8,128]{2,1,0:T(8,128)S(1)}) custom-call(f32[16,128,128]{2,1,0:T(8,128)} %right_ref.1, f32[16,128,128]{2,1,0:T(8,128)} %diag_ref.1, f32[2,24,128]{2,1,0:T(8,128)} %constant.2.clone.table_ref), custom_call_target="tpu_custom_call" | custom-call | tf_op jit(solution)/shard_map/cg/pallas_call | solution.py:567
  37.2 2.3 %combine.1 = (f32[16,128,128]{2,1,0:T(8,128)}, f32[16,128,128]{2,1,0:T(8,128)}) custom-call(f32[11,24,144,128]{3,2,1,0:T(8,128)S(1)} %get-tuple-element.4.V, f32[21,8,128]{2,1,0:T(8,128)S(1)} %get-tuple-element.5.COEF), custom_call_target="tpu_custom_call" | custom-call | tf_op jit(solution)/shard_map/combine/pallas_call | solution.py:596

commit v5 on v4

--- a/solution.py
+++ b/solution.py
@@ -18,6 +18,8 @@
 PAD = 8
 SLOTS = 8
 SHIFT = 32
+WHOLE = 64
+LATE = 16
 MESH = pl.DeviceIdType.MESH
 
 
@@ -39,9 +41,12 @@
     divide = np.zeros((n, n + 1))
     divide[:, 1:] = -np.linalg.inv(apply[1:])
     maps = np.concatenate([divide, np.eye(n + 1), at_zero[None]]).T
-    sides = np.zeros((24, 128))
-    sides[:n, SHIFT : SHIFT + maps.shape[1]] = -maps[:n]
-    sides[16:, SHIFT : SHIFT + maps.shape[1]] = maps[n]
+    sides = np.zeros((32, 128))
+    wide = slice(SHIFT, SHIFT + maps.shape[1])
+    sides[: n - 1, wide] = maps[: n - 1]
+    sides[: n - 1, WHOLE : WHOLE + n - 1] = np.eye(n - 1)
+    sides[16:24, wide] = maps[n - 1]
+    sides[24:, wide] = maps[n]
     high = sides.astype(np.float32)
     return np.stack([high, (sides - high).astype(np.float32)])
 
@@ -418,10 +423,12 @@
         base, steps, near = BASES[index], BLOCKS[index], BLOCKS[index - 1] if index else 0
         final = index + 1 == len(BLOCKS)
         inner(base, steps, near)
-        last = n - 1 if final else base + steps
-        middle_products(base + 1 if index else 0, last, near + steps - final)
         if final:
+            middle_products(base + 1, n - 2, near + steps - 2)
+            middle_products(n - 1, n - 1, near + steps - 1)
             middle_products(n, n, near + steps)
+        else:
+            middle_products(base + 1 if index else 0, base + steps, near + steps)
 
     begin(0)
     for index, (base, steps) in enumerate(zip(BASES, BLOCKS)):
@@ -437,7 +444,8 @@
                 send(index + 1, "v", plane)
             side_products(BASES[index - 1] + 1 if index > 1 else 0, base, 0, near)
             if final:
-                side_products(base + 1, n - 1, steps - 1, steps - 1 + near)
+                side_products(base + 1, n - 2, steps - 2, steps - 2 + near)
+                side_products(n - 1, n - 1, steps - 1, steps - 1 + near)
                 side_products(n, n, steps, steps + near)
             else:
                 side_products(base + 1, base + steps, steps, steps + near)
@@ -457,71 +465,90 @@
                         send(1, "v", plane)
                     begin(1)
             if final:
-                if g < steps:
-                    near = steps - 1 - g
-                    products(
-                        base + 1,
-                        n - 1,
-                        (GHOST + near, GHOST + planes - 1 - near),
-                        planes // 2 - 1 - near,
-                    )
-                near = steps - g
-                products(n, n, (GHOST + near, GHOST + planes - 1 - near), planes // 2 - 1 - near)
-                if g == steps - 1:
+                for back, rows_at in ((2, (base + 1, n - 2)), (1, (n - 1, n - 1)), (0, (n, n))):
+                    near = steps - back - g
+                    if near >= 0:
+                        products(
+                            *rows_at,
+                            (GHOST + near, GHOST + planes - 1 - near),
+                            planes // 2 - 1 - near,
+                        )
+                if g == steps - 2:
+                    m = n - 1
                     where = {
-                        (i, j): sorted({n * i + j, n * j + i}) for i, j in pairs if j < n
+                        (i, j): sorted({m * i + j, m * j + i}) for i, j in pairs if j < m
                     }
-                    share(0, reduce(where, n * n))
+                    share(0, reduce(where, m * m))
         if index:
             for plane in range(min(steps, after)):
                 send(index + 1, "v", plane)
-    share(1, reduce({(i, n): [i] for i in range(n)}, n))
+    late = {(i, n - 1): [i] for i in range(n)}
+    late.update({(i, n): [LATE + i] for i in range(n)})
+    share(1, reduce(late, LATE + n))
     wait_sent()
     wait_shared()
 
     table_load.wait()
+    m = n - 1
     sub = lax.broadcasted_iota(jnp.int32, (8, 128), 0)
+    row = lax.broadcasted_iota(jnp.int32, (16, 128), 0)
+    wide = lax.broadcasted_iota(jnp.int32, (16, 128), 1)
     got = collect(0)
     parts = []
     for h in range(2):
         top, bottom = zero, zero
-        for i in range(n):
-            moved = got[h] if i == 0 else pltpu.roll(got[h], 128 - n * i, 1)
+        for i in range(m):
+            moved = got[h] if i == 0 else pltpu.roll(got[h], 128 - m * i, 1)
             if i < 8:
                 top = jnp.where(sub == i, moved, top)
             else:
                 bottom = jnp.where(sub == i - 8, moved, bottom)
         both = jnp.concatenate([top, bottom], axis=0)
-        wide = lax.broadcasted_iota(jnp.int32, (16, 128), 1)
-        parts.append(jnp.where(wide < n, both, TAB[h, 0:16, :]))
+        parts.append(jnp.where(wide < m, both, TAB[h, 0:16, :]))
     M = tuple(parts)
-    row = lax.broadcasted_iota(jnp.int32, (16, 128), 0)
-    for k in range(n):
-        column = tuple(jnp.broadcast_to(m[:, k : k + 1], (16, 128)) for m in M)
+    for k in range(m):
+        column = tuple(jnp.broadcast_to(v[:, k : k + 1], (16, 128)) for v in M)
         pivot = tuple(jnp.broadcast_to(c[k : k + 1, :], (16, 128)) for c in column)
-        scaled = mul2(tuple(jnp.broadcast_to(m[k : k + 1, :], (16, 128)) for m in M), inverse2(pivot))
+        scaled = mul2(tuple(jnp.broadcast_to(v[k : k + 1, :], (16, 128)) for v in M), inverse2(pivot))
         rest = add2(M, neg2(mul2(column, scaled)))
-        M = tuple(jnp.where(row == k, s, m) for s, m in zip(scaled, rest))
+        M = tuple(jnp.where(row == k, s, v) for s, v in zip(scaled, rest))
+    M = tuple(jnp.where(row < m, v, 0.0) for v in M)
     got = collect(1)
-    wide = lax.broadcasted_iota(jnp.int32, (16, 128), 1)
-    H = tuple(
-        jnp.broadcast_to(
-            jnp.sum(
-                jnp.where(wide == row, jnp.concatenate([v, v], axis=0), 0.0), axis=1, keepdims=True
-            ),
-            (16, 128),
-        )
-        for v in got
-    )
-    H = tuple(jnp.where(row < n, v, 0.0) for v in H)
-    M = tuple(jnp.where(row < n, m, 0.0) for m in M)
-    terms = mul2(M, H)
-    terms = sublanes2(add2(tuple(t[0:8] for t in terms), tuple(t[8:16] for t in terms)))
-    terms = add2(terms, (TAB[0, 16:24, :], TAB[1, 16:24, :]))
-    value = tuple(
-        jnp.broadcast_to(t[:, SHIFT + 2 * n + 1 : SHIFT + 2 * n + 2], (8, 128)) for t in terms
-    )
-    terms = mul2(terms, inverse2(value))
+
+    def down(pair, lane0):
+        return tuple(
+            jnp.broadcast_to(
+                jnp.sum(
+                    jnp.where(
+                        jnp.logical_and(wide == row + lane0, row < m),
+                        jnp.concatenate([v, v], axis=0),
+                        0.0,
+                    ),
+                    axis=1,
+                    keepdims=True,
+                ),
+                (16, 128),
+            )
+            for v in pair
+        )
+
+    def over_rows(pair):
+        return sublanes2(add2(tuple(t[0:8] for t in pair), tuple(t[8:16] for t in pair)))
+
+    def at_lane(pair, k):
+        return tuple(jnp.broadcast_to(t[:, k : k + 1], (8, 128)) for t in pair)
+
+    near_last, last_column = down(got, 0), down(got, LATE)
+    corner, side = at_lane(got, m), at_lane(got, LATE + m)
+    first, second = over_rows(mul2(M, near_last)), over_rows(mul2(M, last_column))
+    image = down(first, WHOLE)
+    pivot = add2(corner, neg2(over_rows(mul2(image, near_last))))
+    value = add2(side, neg2(over_rows(mul2(image, last_column))))
+    share_last = mul2(value, inverse2(pivot))
+    edge = add2(tuple(TAB[h, 16:24, :] for h in range(2)), neg2(first))
+    terms = add2(tuple(TAB[h, 24:32, :] for h in range(2)), neg2(second))
+    terms = add2(terms, neg2(mul2(edge, share_last)))
+    terms = mul2(terms, inverse2(at_lane(terms, SHIFT + 2 * n + 1)))
     factor = terms[0]
     for i in range(2 * n + 1):
         COEF[i] = jnp.broadcast_to(factor[:, SHIFT + i : SHIFT + i + 1], (8, 128))
@@ -576,7 +603,7 @@
             pltpu.VMEM((2, 128, 128), f32),
             pltpu.VMEM((2, 2, 128), f32),
             pltpu.VMEM((2, devices, 2, 128), f32),
-            pltpu.VMEM((2, 24, 128), f32),
+            pltpu.VMEM((2, 32, 128), f32),
             dma((7,)),
             dma((2,)),
             dma((2, MESSAGES)),

time: 39.7 us -> 39 us (0.982)
  Pallas kernels: 38.9 us -> 38.2 us
    pallas_call x1, Pallas kernels: 36.6 us -> 35.9 us  [local(): pl.pallas_call(functools.partial(kernel, devices), out_shape=held, in_spe...]
where the time goes in v5:
time: 39 us; the launch traced here: 38.8 us
  Pallas kernels  38.2 us (98%)
  between operations  0.64 us (2%)
    pallas_call x1, Pallas kernels, local(): pl.pallas_call(functools.partial(kernel, devices), out_shape=held, in_spe...  35.9 us
    pallas_call x1, Pallas kernels, local(): pl.pallas_call(combine_kernel, out_shape=(out, out), in_specs=[pl.BlockSp...  2.34 us

profile of v5, /device:TPU:0, one launch (start us, length us, event | category | flops | bytes accessed | tf_op | source)
XLA Modules:
  0.0 38.8 jit_solution(3629385922917495669)
XLA Ops:
  0.6 35.9 %cg.1 = (f32[11,24,144,128]{3,2,1,0:T(8,128)S(1)}, f32[21,8,128]{2,1,0:T(8,128)S(1)}) custom-call(f32[16,128,128]{2,1,0:T(8,128)} %right_ref.1, f32[16,128,128]{2,1,0:T(8,128)} %diag_ref.1, f32[2,32,128]{2,1,0:T(8,128)} %constant.2.clone.table_ref), custom_call_target="tpu_custom_call" | custom-call | tf_op jit(solution)/shard_map/cg/pallas_call | solution.py:594
  36.5 2.3 %combine.1 = (f32[16,128,128]{2,1,0:T(8,128)}, f32[16,128,128]{2,1,0:T(8,128)}) custom-call(f32[11,24,144,128]{3,2,1,0:T(8,128)S(1)} %get-tuple-element.4.V, f32[21,8,128]{2,1,0:T(8,128)S(1)} %get-tuple-element.5.COEF), custom_call_target="tpu_custom_call" | custom-call | tf_op jit(solution)/shard_map/combine/pallas_call | solution.py:623

commit v6 on v5

--- a/solution.py
+++ b/solution.py
@@ -569,10 +569,10 @@
         return 0
 
     copies = []
-    group = 2
-    for q in range(planes // group):
-        lax.fori_loop(group * q, group * q + group, one, 0)
-        at = pl.ds(group * q, group)
+    edges = list(range(0, planes - 1, 2)) + [planes - 1, planes]
+    for q, (first, last) in enumerate(zip(edges[:-1], edges[1:])):
+        lax.fori_loop(first, last, one, 0)
+        at = pl.ds(first, last - first)
         for k, (source, target) in enumerate(((X, x_out), (R, r_out))):
             copies.append(pltpu.make_async_copy(source.at[at], target.at[at], sem.at[k, q]))
             copies[-1].start()
@@ -628,7 +628,7 @@
         scratch_shapes=[
             pltpu.VMEM(right_side.shape, f32),
             pltpu.VMEM(right_side.shape, f32),
-            dma((2, planes // 2)),
+            dma((2, planes // 2 + 1)),
         ],
         compiler_params=pltpu.CompilerParams(vmem_limit_bytes=8 * 2**20),
         name="combine",

time: 39 us -> 38.9 us (level)
  no operation moved by 1% of the time
where the time goes in v6:
time: 38.9 us; the launch traced here: 38.8 us
  Pallas kernels  38.2 us (98%)
  between operations  0.64 us (2%)
    pallas_call x1, Pallas kernels, local(): pl.pallas_call(functools.partial(kernel, devices), out_shape=held, in_spe...  35.9 us
    pallas_call x1, Pallas kernels, local(): pl.pallas_call(combine_kernel, out_shape=(out, out), in_specs=[pl.BlockSp...  2.3 us

profile of v6, /device:TPU:0, one launch (start us, length us, event | category | flops | bytes accessed | tf_op | source)
XLA Modules:
  0.0 38.8 jit_solution(5071737838232022102)
XLA Ops:
  0.6 35.9 %cg.1 = (f32[11,24,144,128]{3,2,1,0:T(8,128)S(1)}, f32[21,8,128]{2,1,0:T(8,128)S(1)}) custom-call(f32[16,128,128]{2,1,0:T(8,128)} %right_ref.1, f32[16,128,128]{2,1,0:T(8,128)} %diag_ref.1, f32[2,32,128]{2,1,0:T(8,128)} %constant.2.clone.table_ref), custom_call_target="tpu_custom_call" | custom-call | tf_op jit(solution)/shard_map/cg/pallas_call | solution.py:594
  36.5 2.3 %combine.1 = (f32[16,128,128]{2,1,0:T(8,128)}, f32[16,128,128]{2,1,0:T(8,128)}) custom-call(f32[11,24,144,128]{3,2,1,0:T(8,128)S(1)} %get-tuple-element.4.V, f32[21,8,128]{2,1,0:T(8,128)S(1)} %get-tuple-element.5.COEF), custom_call_target="tpu_custom_call" | custom-call | tf_op jit(solution)/shard_map/combine/pallas_call | solution.py:623
